TPU v7x, 256 devices: a whole 4x4x8 slice. The times are simulated.
256 devices in a mesh: section: 8 (over z), ctx: 32 (over x, y, core).
Axes of the slice: x: 4, y: 4, z: 8, core: 2. Of those that a mesh axis runs over, the one named last changes fastest.
Arguments:
- queries: bfloat16 [8, 8192, 3072], P('section', 'ctx'), may hold values from -160 to 160
- keys: bfloat16 [8, 8192, 512], P('section', 'ctx'), may hold values from -48 to 48
- values: bfloat16 [8, 8192, 512], P('section', 'ctx'), may hold values from -15 to 15
- cotangent: bfloat16 [8, 8192, 3072], P('section', 'ctx'), may hold values from -6 to 6
- router_logits: bfloat16 [8, 8192], P('section', 'ctx'), may hold values from -8 to 8
- positions: int32 [8, 8192], P('section', 'ctx'), may hold values from -1 to 32767, as said below
- counts: int32 [8, 32], P('section', 'ctx'), may hold values from 0 to 2, as said below
Outputs:
- handed: bfloat16 [8, 8192, 3072], P('section', 'ctx')
- value_grad: bfloat16 [8, 8192, 512], P('section', 'ctx')
- gate_grad: bfloat16 [8, 8192], P('section', 'ctx')
Inputs may be any that keep to these rules, and one draw needn't show every extreme that they name: For every micro-batch and every shard c, the counts of shards 0 to c sum to c + 1 or c + 2; shard 0 holds 2 blocks; all counts of a micro-batch sum to 32. In shard c's slots, the first counts * 128 hold distinct positions in increasing order, all within c * 1024 to (c + 1) * 1024 - 1; the other slots hold -1.
All inputs are finite; a program needn't handle non-finite values.
Results may differ from a plain program's by a relative error of at most 0.0066.
Values may be sent and summed in bfloat16 or wider, within the bound.
A program may use at most 128 MiB of HBM per device.

v0:
```python
import math

import jax
import jax.numpy as jnp
from jax import lax
from jax.sharding import PartitionSpec as P

QUERY_HEADS = 24
KEY_VALUE_HEADS = 4
HEAD_SIZE = 128
BLOCK_ROWS = 128
MAXB = 2


score_masked_out = -1e30


def copy_for_each(x, axis):
    copies = jnp.broadcast_to(x, (lax.axis_size(axis), *x.shape))
    return lax.all_to_all(copies, axis, split_axis=0, concat_axis=0, tiled=True)


def folded_in_pairs(pieces, combine):
    while len(jax.tree.leaves(pieces)[0]) > 1:
        pieces = jax.vmap(combine)(*(pieces[side::2] for side in (0, 1)))
    return pieces[0]


def carried_in(x, axis, combine, identity):
    devices, mine = (lax.axis_size(axis), lax.axis_index(axis))
    passed = jnp.arange(devices) < mine

    def kept(part, zero, own):
        part = jnp.where(
            passed.reshape(-1, *(1 for _ in own.shape)), part, jnp.asarray(zero, own.dtype)
        )
        return part

    pieces = copy_for_each(x, axis)
    return folded_in_pairs(kept(pieces, identity, x), combine)


def passed_along(block, axis, distance):
    devices = range(lax.axis_size(axis))
    route = [(i - distance, i) for i in devices if i - distance in devices]
    return lax.ppermute(block, axis, route)


def sent_together(arrays, axis, dim, along):
    widths = [a.shape[along] for a in arrays]
    both = jnp.concatenate(arrays, axis=along)
    out = lax.all_gather(both, axis, axis=dim, tiled=True)
    return tuple(jnp.split(out, [sum(widths[:k]) for k in range(1, len(widths))], axis=along))


def for_sending(x):

    def short(part):
        return part.astype(jnp.bfloat16) if part.dtype == jnp.float32 else part

    return jax.tree.map(short, x)


def in_blocks(x, dim, devices):
    before, after = (x.shape[:dim], x.shape[dim + 1 :])
    return jnp.moveaxis(x.reshape(*before, devices, -1, *after), dim, 0)


def sent_and_summed(x, axis, dim):
    devices = lax.axis_size(axis)
    tiles = lax.all_to_all(in_blocks(x, dim, devices), axis, 0, 0, tiled=True)
    return jnp.sum(tiles.astype(jnp.float32), axis=0)


def from_behind(x, axis, by):
    devices = lax.axis_size(axis)
    return lax.ppermute(x, axis, [(i, (i + by) % devices) for i in range(devices)])


def add_ints(earlier, later):
    return earlier + later


def local(queries, keys, values, cotangent, router_logits, positions, counts):
    query_group_width = QUERY_HEADS // KEY_VALUE_HEADS
    shards = lax.axis_size("ctx")
    key_width = BLOCK_ROWS * min(shards, max(1, 512 // BLOCK_ROWS))
    score_scale = 1.0 / math.sqrt(HEAD_SIZE)
    blocks_held = counts[0, 0]
    before = carried_in(blocks_held - 1, "ctx", add_ints, jnp.int32(0))
    carried = before + blocks_held - 1
    last_block = jnp.maximum(blocks_held - 1, 0)
    own_arrays = (queries[0], keys[0], values[0], cotangent[0], router_logits[0], positions[0])
    outgoing = [
        lax.dynamic_slice_in_dim(source, last_block * BLOCK_ROWS, BLOCK_ROWS, 0)
        for source in own_arrays
    ]
    incoming = passed_along(
        (outgoing[0], outgoing[1], outgoing[2], outgoing[3], outgoing[4], outgoing[5]), "ctx", 1
    )
    received_one = before == 1
    chosen = [
        jnp.where(received_one, arriving, source[:BLOCK_ROWS])
        for arriving, source in zip(incoming, own_arrays)
    ]
    query_row_block, key_row_block, value_rows, grad_rows, logit_rows, place_rows = chosen
    gate_values = jax.nn.sigmoid(logit_rows.astype(jnp.float32))
    query_head_rows = query_row_block.reshape(
        BLOCK_ROWS, KEY_VALUE_HEADS, query_group_width, HEAD_SIZE
    )
    latest_query = jnp.max(place_rows)

    def split_width():
        return key_width

    def scores_for(key_portion, place_part):
        local_row_count = key_portion.shape[0]
        scores = (
            jnp.einsum(
                "qhgd,khd->hgqk",
                query_head_rows,
                key_portion.reshape(local_row_count, KEY_VALUE_HEADS, HEAD_SIZE),
                preferred_element_type=jnp.float32,
            )
            * score_scale
        )
        allowed = place_part[None, :] <= place_rows[:, None]
        return (scores, allowed)

    def absorb_part(running, key_portion, value_portion, place_part):
        row_top, weight_sum, summed = running
        local_row_count = key_portion.shape[0]
        scores, allowed = scores_for(key_portion, place_part)
        new_top = jnp.maximum(
            row_top, jnp.max(jnp.where(allowed, scores, score_masked_out), axis=-1)
        )
        weights = jnp.where(allowed, jnp.exp(scores - new_top[..., None]), 0.0)
        factor = jnp.exp(row_top - new_top)
        weight_sum = weight_sum * factor + jnp.sum(weights, axis=-1)
        summed = summed * factor[..., None] + jnp.einsum(
            "hgqk,khd->hgqd",
            weights.astype(jnp.bfloat16),
            value_portion.reshape(local_row_count, KEY_VALUE_HEADS, HEAD_SIZE),
            preferred_element_type=jnp.float32,
        )
        return (new_top, weight_sum, summed)

    def absorb(running, key_portion, value_portion, place_part):
        return lax.cond(
            jnp.min(place_part) > latest_query,
            lambda: running,
            lambda: absorb_part(running, key_portion, value_portion, place_part),
        )

    start_state = (
        jnp.full((KEY_VALUE_HEADS, query_group_width, BLOCK_ROWS), score_masked_out, jnp.float32),
        jnp.zeros((KEY_VALUE_HEADS, query_group_width, BLOCK_ROWS), jnp.float32),
        jnp.zeros((KEY_VALUE_HEADS, query_group_width, BLOCK_ROWS, HEAD_SIZE), jnp.float32),
    )
    collected_rows = (
        *sent_together((key_row_block, value_rows), "ctx", 0, 1),
        lax.all_gather(for_sending(place_rows), "ctx", axis=0, tiled=True).astype(place_rows.dtype),
    )
    key_complete = collected_rows[0]
    local_row_count = key_complete.shape[0]
    rows_per_step = split_width()
    relay_step_count = local_row_count // rows_per_step
    stacked = (
        key_complete.reshape(relay_step_count, rows_per_step, KEY_VALUE_HEADS * HEAD_SIZE),
        collected_rows[1].reshape(relay_step_count, rows_per_step, KEY_VALUE_HEADS * HEAD_SIZE),
        collected_rows[2].reshape(relay_step_count, rows_per_step),
    )

    def visit(state_in, member):
        return (absorb(state_in, member[0], member[1], member[2]), None)

    final_state = lax.scan(visit, start_state, stacked)[0]
    row_top, weight_sum, summed = final_state
    attended = jnp.transpose(summed / weight_sum[..., None], (2, 0, 1, 3)).reshape(
        BLOCK_ROWS, QUERY_HEADS * HEAD_SIZE
    )
    log_total = row_top + jnp.log(weight_sum)
    gradient_broad = grad_rows.astype(jnp.float32)
    output_gradient = (
        (gate_values[:, None] * gradient_broad)
        .astype(jnp.bfloat16)
        .reshape(BLOCK_ROWS, KEY_VALUE_HEADS, query_group_width, HEAD_SIZE)
    )

    def value_portion(key_portion, place_part):
        local_row_count = key_portion.shape[0]
        scores, allowed = scores_for(key_portion, place_part)
        probabilities = jnp.where(allowed, jnp.exp(scores - log_total[..., None]), 0.0).astype(
            jnp.bfloat16
        )
        return jnp.einsum(
            "hgqk,qhgd->khd", probabilities, output_gradient, preferred_element_type=jnp.float32
        ).reshape(local_row_count, KEY_VALUE_HEADS * HEAD_SIZE)

    def value_block(key_portion, place_part):
        return lax.cond(
            jnp.min(place_part) > latest_query,
            lambda: jnp.zeros((key_portion.shape[0], KEY_VALUE_HEADS * HEAD_SIZE), jnp.float32),
            lambda: value_portion(key_portion, place_part),
        )

    key_portion = collected_rows[0]
    place_part = collected_rows[2]
    local_row_count = key_portion.shape[0]
    rows_per_step = split_width()
    relay_step_count = local_row_count // rows_per_step
    product_terms = lax.map(
        lambda member: value_block(member[0], member[1]),
        (
            key_portion.reshape(relay_step_count, rows_per_step, KEY_VALUE_HEADS * HEAD_SIZE),
            place_part.reshape(relay_step_count, rows_per_step),
        ),
    )
    value_sum = sent_and_summed(
        product_terms.reshape(local_row_count, KEY_VALUE_HEADS * HEAD_SIZE).astype(jnp.bfloat16),
        "ctx",
        0,
    )
    branch = (gate_values[:, None] * attended).astype(jnp.bfloat16)
    gate_term = (
        gate_values * (1.0 - gate_values) * jnp.sum(gradient_broad * attended, axis=1)
    ).astype(jnp.bfloat16)
    value_finished = value_sum.astype(jnp.bfloat16)
    returned = passed_along((branch, value_finished, gate_term), "ctx", -1)
    local_results = (branch, value_finished, gate_term)
    slot_lists = ([], [], [])
    for slot_index in range(MAXB):
        local_slot = jnp.logical_and(before == 0, slot_index == 0)
        back_slot = jnp.logical_and(carried == 1, blocks_held - 1 == slot_index)
        for member_index in range(3):
            mine = local_results[member_index]
            filled = jnp.where(
                local_slot, mine, jnp.where(back_slot, returned[member_index], jnp.zeros_like(mine))
            )
            slot_lists[member_index].append(filled)
    owner_branch = jnp.concatenate(slot_lists[0], axis=0)
    value_grad = jnp.concatenate(slot_lists[1], axis=0)
    gate_grad = jnp.concatenate(slot_lists[2], axis=0)
    handed = from_behind(owner_branch, "section", 1)
    return (handed[None], value_grad[None], gate_grad[None])


def solution(mesh):
    return jax.shard_map(
        local,
        mesh=mesh,
        in_specs=(
            P("section", "ctx", None),
            P("section", "ctx", None),
            P("section", "ctx", None),
            P("section", "ctx", None),
            P("section", "ctx"),
            P("section", "ctx"),
            P("section", "ctx"),
        ),
        out_specs=(P("section", "ctx", None), P("section", "ctx", None), P("section", "ctx")),
        check_vma=False,
    )
```

profile of v0, /device:TPU:2, one launch (start us, length us, event | category | flops | bytes accessed | tf_op | source)
XLA Modules:
  0.0 348.9 jit_solution(6655201932795278297)
XLA Ops:
  8.4 7.6 %all-to-all-start = ((s32[32,1,1]{2,1,0:T(1,128)}), s32[32,1,1]{2,1,0:T(1,128)S(1)}, u32[]{:S(2)}, u32[]{:S(2)}) async-start(s32[32,1,1]{2,1,0:T(1,128)} %broadcast_in_dim.73), calls=%async_computation | async-start | bytes 32768 | tf_op jit(solution)/shard_map/all_to_all | solution.py:20
  20.0 3.4 collective-permute-start.2
  35.2 3.0 collective-permute-start.1
  41.4 3.1 collective-permute-start
  45.3 4.7 %collective-permute-done.1 = s32[128]{0:T(128)S(1)} collective-permute-done((s32[128]{0:T(128)S(1)}, s32[128]{0:T(128)S(1)}, u32[]{:S(2)}, u32[]{:S(2)}) %collective-permute-start.1) | collective-permute-done | bytes 544 | tf_op jit(solution)/shard_map/ppermute | solution.py:46
  50.6 22.1 %all-gather = s32[32,1,128]{2,1,0:T(1,128)S(1)} all-gather(s32[1,1,128]{2,1,0:T(1,128)S(1)} %bitcast.117), channel_id=1, replica_groups=mesh['section'=8,'ctx'=32] {'ctx'}, dimensions={0}, use_global_device_ids=true | all-gather | bytes 16896 | tf_op jit(solution)/shard_map/all_gather | solution.py:162
  74.4 20.7 %all-gather.3.cloned.1.call-done = bf16[4096,1024]{1,0:T(8,128)(2,1)} async-done(((bf16[128,1024]{1,0:T(8,128)(2,1)}), bf16[4096,1024]{1,0:T(8,128)(2,1)}) %all-gather.3.cloned.1.call-update) | async-done | bytes 8388624 | tf_op jit(solution)/shard_map/all_gather | solution.py:52
  95.0 5.8 %fusion.38 = (bf16[4096,512]{1,0:T(8,128)(2,1)}, bf16[4096,512]{1,0:T(8,128)(2,1)}) fusion(bf16[4096,1024]{1,0:T(8,128)(2,1)} %all-gather.3.cloned.1.call-done), kind=kLoop, calls=%fused_computation.78 | loop fusion | bytes 16777216 | tf_op jit(solution)/shard_map/split | solution.py:53
  100.8 6.4 %copy.83 = bf16[8,512,512]{1,2,0:T(8,128)(2,1)} copy(bf16[8,512,512]{2,1,0:T(8,128)(2,1)} %bitcast.106) | data formatting | bytes 8388608 | tf_op jit(solution)/shard_map/while | solution.py:177
  107.2 6.5 %copy.85 = bf16[8,512,512]{1,2,0:T(8,128)(2,1)} copy(bf16[8,512,512]{2,1,0:T(8,128)(2,1)} %bitcast.105) | data formatting | bytes 8388608 | tf_op jit(solution)/shard_map/while | solution.py:177
  113.9 34.6 %while.24 = (s32[]{:T(128)}, f32[4,6,128]{2,1,0:T(8,128)S(1)}, f32[4,6,128]{2,1,0:T(8,128)S(1)}, f32[4,6,128,128]{3,2,1,0:T(8,128)S(1)}, s32[8,512]{1,0:T(8,128)...) while((s32[]{:T(128)}, f32[4,6,128]{2,1,0:T(8,128)S(1)}, ...), condition=%wide.region_7.8_spmd, body=%wide.region_1.7_spmd.sunk | while | flops 823466496 | bytes 26417920 | solution.py:177
  115.9 6.3 %conditional.4 = (f32[4,6,128]{2,1,0:T(8,128)S(1)}, f32[4,6,128]{2,1,0:T(8,128)S(1)}, f32[4,6,128,128]{3,2,1,0:T(8,128)S(1)}) conditional(s32[]{:T(128)} %convert_element_type.71, (s32[1,512]{1,0:T(1,128)S(1)}, s32[128]{0:T(128)S(1)}, bf16[8,512,512]{1,2,0:T(8,128)(2,1)}, s32[]{:T(128)}, bf16[128,4,6,128]{3,0,2,1:T(8,128)(2,1)S(1)}, ...), branch_computations={%region_3.5_spmd, %region_6.6_spmd} | conditional | flops 823465984 | bytes 26389020 | solution.py:149
  124.1 6.3 %conditional.4 = (f32[4,6,128]{2,1,0:T(8,128)S(1)}, f32[4,6,128]{2,1,0:T(8,128)S(1)}, f32[4,6,128,128]{3,2,1,0:T(8,128)S(1)}) conditional(s32[]{:T(128)} %convert_element_type.71, (s32[1,512]{1,0:T(1,128)S(1)}, s32[128]{0:T(128)S(1)}, bf16[8,512,512]{1,2,0:T(8,128)(2,1)}, s32[]{:T(128)}, bf16[128,4,6,128]{3,0,2,1:T(8,128)(2,1)S(1)}, ...), branch_computations={%region_3.5_spmd, %region_6.6_spmd} | conditional | flops 823465984 | bytes 26389020 | solution.py:149
  132.3 6.3 %conditional.4 = (f32[4,6,128]{2,1,0:T(8,128)S(1)}, f32[4,6,128]{2,1,0:T(8,128)S(1)}, f32[4,6,128,128]{3,2,1,0:T(8,128)S(1)}) conditional(s32[]{:T(128)} %convert_element_type.71, (s32[1,512]{1,0:T(1,128)S(1)}, s32[128]{0:T(128)S(1)}, bf16[8,512,512]{1,2,0:T(8,128)(2,1)}, s32[]{:T(128)}, bf16[128,4,6,128]{3,0,2,1:T(8,128)(2,1)S(1)}, ...), branch_computations={%region_3.5_spmd, %region_6.6_spmd} | conditional | flops 823465984 | bytes 26389020 | solution.py:149
  153.0 34.9 %while.25 = (s32[]{:T(128)}, bf16[8,512,512]{2,1,0:T(8,128)(2,1)}, s32[8,512]{1,0:T(8,128)S(1)}, s32[]{:T(128)}, s32[128]{0:T(128)S(1)}, /*index=5*/bf16[8,512,5...) while((s32[]{:T(128)}, bf16[8,512,512]{2,1,0:T(8,128)(2,1)}, ...), condition=%wide.region_12.13_spmd, body=%wide.region_8.12_spmd.sunk | while | flops 811663872 | bytes 5917887 | solution.py:212
  154.9 3.6 %conditional.5 = (bf16[1,512,512]{1,2,0:T(8,128)(2,1)S(1)}) conditional(s32[]{:T(128)} %convert_element_type.72, (s32[1,512]{1,0:T(1,128)S(1)}, s32[128]{0:T(128)S(1)}, bf16[8,512,512]{1,2,0:T(8,128)(2,1)}, s32[]{:T(128)}, bf16[128,4,6,128]{3,0,2,1:T(8,128)(2,1)S(1)}, /*index=5*/f32[4,6,128]{2,1,0:T(8,128)S(1)}, ...), branch_computations={%region_10.10_spmd, %region_11.11_spmd} | conditional | flops 811663360 | bytes 3815948 | solution.py:201
  161.5 3.6 %conditional.5 = (bf16[1,512,512]{1,2,0:T(8,128)(2,1)S(1)}) conditional(s32[]{:T(128)} %convert_element_type.72, (s32[1,512]{1,0:T(1,128)S(1)}, s32[128]{0:T(128)S(1)}, bf16[8,512,512]{1,2,0:T(8,128)(2,1)}, s32[]{:T(128)}, bf16[128,4,6,128]{3,0,2,1:T(8,128)(2,1)S(1)}, /*index=5*/f32[4,6,128]{2,1,0:T(8,128)S(1)}, ...), branch_computations={%region_10.10_spmd, %region_11.11_spmd} | conditional | flops 811663360 | bytes 3815948 | solution.py:201
  168.1 3.6 %conditional.5 = (bf16[1,512,512]{1,2,0:T(8,128)(2,1)S(1)}) conditional(s32[]{:T(128)} %convert_element_type.72, (s32[1,512]{1,0:T(1,128)S(1)}, s32[128]{0:T(128)S(1)}, bf16[8,512,512]{1,2,0:T(8,128)(2,1)}, s32[]{:T(128)}, bf16[128,4,6,128]{3,0,2,1:T(8,128)(2,1)S(1)}, /*index=5*/f32[4,6,128]{2,1,0:T(8,128)S(1)}, ...), branch_computations={%region_10.10_spmd, %region_11.11_spmd} | conditional | flops 811663360 | bytes 3815948 | solution.py:201
  187.9 56.3 %all-to-all-start.1 = ((bf16[32,128,512]{2,1,0:T(8,128)(2,1)}), bf16[32,128,512]{2,1,0:T(8,128)(2,1)}, u32[]{:S(2)}, u32[]{:S(2)}) async-start(bf16[32,128,512]{2,1,0:T(8,128)(2,1)} %bitcast.110), calls=%async_computation.1 | async-start | bytes 8388608 | tf_op jit(solution)/shard_map/all_to_all | solution.py:71
  244.2 4.3 %collective-permute-start.5 = (bf16[128,3072]{0,1:T(8,128)(2,1)S(1)}, bf16[128,3072]{0,1:T(8,128)(2,1)S(1)}, u32[]{:S(2)}, u32[]{:S(2)}) collective-permute-start(bf16[128,3072]{0,1:T(8,128)(2,1)S(1)} %get-tuple-element.429), channel_id=1, source_target_pairs={{1,0},{2,1},{3,2},{4,3},{5,4},{6,5},{7,6},{8,7},{9,8},{10,9},{11,1... | collective-permute-start | bytes 2359304 | tf_op jit(solution)/shard_map/ppermute | solution.py:46
  248.6 53.3 %collective-permute-done.5 = bf16[128,3072]{0,1:T(8,128)(2,1)S(1)} collective-permute-done((bf16[128,3072]{0,1:T(8,128)(2,1)S(1)}, bf16[128,3072]{0,1:T(8,128)(2,1)S(1)}, u32[]{:S(2)}, u32[]{:S(2)}) %collective-permute-start.5) | collective-permute-done | bytes 786464 | tf_op jit(solution)/shard_map/ppermute | solution.py:46
  303.1 5.7 %collective-permute-start.9 = (bf16[128]{0:T(256)(128)(2,1)S(1)}, bf16[128]{0:T(256)(128)(2,1)S(1)}, u32[]{:S(2)}, u32[]{:S(2)}) collective-permute-start(bf16[128]{0:T(256)(128)(2,1)S(1)} %get-tuple-element.408), channel_id=1, source_target_pairs={{1,0},{2,1},{3,2},{4,3},{5,4},{6,5},{7,6},{8,7},{9,8},{10,9},{11,1... | collective-permute-start | bytes 776 | tf_op jit(solution)/shard_map/ppermute | solution.py:46
  308.8 2.8 reduce_sum.32
  314.2 25.4 %collective-permute-done.6 = bf16[256,3072]{0,1:T(8,128)(2,1)S(1)} collective-permute-done((bf16[256,3072]{0,1:T(8,128)(2,1)S(1)}, bf16[256,3072]{0,1:T(8,128)(2,1)S(1)}, u32[]{:S(2)}, u32[]{:S(2)}) %collective-permute-start.6) | collective-permute-done | bytes 1572896 | tf_op jit(solution)/shard_map/ppermute | solution.py:77
  (162 shorter events, 80.6 us)
Async XLA Ops:
  8.4 15.0 %all-to-all-start = ((s32[32,1,1]{2,1,0:T(1,128)}), s32[32,1,1]{2,1,0:T(1,128)S(1)}, u32[]{:S(2)}, u32[]{:S(2)}) async-start(s32[32,1,1]{2,1,0:T(1,128)} %broadcast_in_dim.73), calls=%async_computation | async-start | bytes 32768 | tf_op jit(solution)/shard_map/all_to_all | solution.py:20
  16.1 79.0 %all-gather.3.cloned.1.call-start = ((), (), s32[]{:S(2)}) async-start(), calls=%async_computation.2 | async-start | bytes 8650752 | tf_op jit(solution)/shard_map/all_gather | solution.py:52
  17.0 9.8 %collective-permute-start.3 = (bf16[128,512]{1,0:T(8,128)(2,1)S(1)}, bf16[128,512]{1,0:T(8,128)(2,1)S(1)}, u32[]{:S(2)}, u32[]{:S(2)}) collective-permute-start(bf16[128,512]{1,0:T(8,128)(2,1)S(1)} %dynamic-slice_bitcast_fusion), channel_id=1, source_target_pairs={{0,1},{1,2},{2,3},{3,4},{4,5},{5,6},{6,7},{7,8},{8,9},{9,10},{10,1... | collective-permute-start | bytes 393224 | tf_op jit(solution)/shard_map/ppermute | solution.py:46
  20.0 8.4 %collective-permute-start.2 = (bf16[128,512]{1,0:T(8,128)(2,1)S(1)}, bf16[128,512]{1,0:T(8,128)(2,1)S(1)}, u32[]{:S(2)}, u32[]{:S(2)}) collective-permute-start(bf16[128,512]{1,0:T(8,128)(2,1)S(1)} %dynamic-slice_bitcast_fusion.1), channel_id=1, source_target_pairs={{0,1},{1,2},{2,3},{3,4},{4,5},{5,6},{6,7},{7,8},{8,9},{9,10},{10,1... | collective-permute-start | bytes 393224 | tf_op jit(solution)/shard_map/ppermute | solution.py:46
  30.0 5.2 %copy-start = (s32[1,256]{1,0:T(1,128)S(1)}, s32[1,256]{1,0:T(1,128)}, u32[]{:S(2)}) copy-start(s32[1,256]{1,0:T(1,128)} %param.20) | copy-start | bytes 3076
  30.1 11.3 %copy-start.1 = (bf16[1,256]{1,0:T(2,128)(2,1)S(1)}, bf16[1,256]{1,0:T(2,128)(2,1)}, u32[]{:S(2)}) copy-start(bf16[1,256]{1,0:T(2,128)(2,1)} %param.19) | copy-start | bytes 1540
  33.3 40.6 %collective-permute-start.4 = (bf16[128,3072]{0,1:T(8,128)(2,1)}, bf16[128,3072]{0,1:T(8,128)(2,1)}, u32[]{:S(2)}, u32[]{:S(2)}) collective-permute-start(bf16[128,3072]{0,1:T(8,128)(2,1)} %bitcast.114), channel_id=1, source_target_pairs={{0,1},{1,2},{2,3},{3,4},{4,5},{5,6},{6,7},{7,8},{8,9},{9,10},{10,1... | collective-permute-start | bytes 2359304 | tf_op jit(solution)/shard_map/ppermute | solution.py:46
  35.2 14.7 %collective-permute-start.1 = (s32[128]{0:T(128)S(1)}, s32[128]{0:T(128)S(1)}, u32[]{:S(2)}, u32[]{:S(2)}) collective-permute-start(s32[128]{0:T(128)S(1)} %fusion.33), channel_id=1, source_target_pairs={{0,1},{1,2},{2,3},{3,4},{4,5},{5,6},{6,7},{7,8},{8,9},{9,10},{10,1... | collective-permute-start | bytes 1544 | tf_op jit(solution)/shard_map/ppermute | solution.py:46
  39.4 112.4 %collective-permute-start.7 = (bf16[128,3072]{0,1:T(8,128)(2,1)}, bf16[128,3072]{0,1:T(8,128)(2,1)}, u32[]{:S(2)}, u32[]{:S(2)}) collective-permute-start(bf16[128,3072]{0,1:T(8,128)(2,1)} %bitcast.33), channel_id=1, source_target_pairs={{0,1},{1,2},{2,3},{3,4},{4,5},{5,6},{6,7},{7,8},{8,9},{9,10},{10,1... | collective-permute-start | bytes 2359304 | tf_op jit(solution)/shard_map/ppermute | solution.py:46
  41.4 111.0 %collective-permute-start = (bf16[128]{0:T(256)(128)(2,1)S(1)}, bf16[128]{0:T(256)(128)(2,1)S(1)}, u32[]{:S(2)}, u32[]{:S(2)}) collective-permute-start(bf16[128]{0:T(256)(128)(2,1)S(1)} %fusion.32), channel_id=1, source_target_pairs={{0,1},{1,2},{2,3},{3,4},{4,5},{5,6},{6,7},{7,8},{8,9},{9,10},{10,1... | collective-permute-start | bytes 776 | tf_op jit(solution)/shard_map/ppermute | solution.py:46
  187.9 120.9 %all-to-all-start.1 = ((bf16[32,128,512]{2,1,0:T(8,128)(2,1)}), bf16[32,128,512]{2,1,0:T(8,128)(2,1)}, u32[]{:S(2)}, u32[]{:S(2)}) async-start(bf16[32,128,512]{2,1,0:T(8,128)(2,1)} %bitcast.110), calls=%async_computation.1 | async-start | bytes 8388608 | tf_op jit(solution)/shard_map/all_to_all | solution.py:71
  244.2 57.7 %collective-permute-start.5 = (bf16[128,3072]{0,1:T(8,128)(2,1)S(1)}, bf16[128,3072]{0,1:T(8,128)(2,1)S(1)}, u32[]{:S(2)}, u32[]{:S(2)}) collective-permute-start(bf16[128,3072]{0,1:T(8,128)(2,1)S(1)} %get-tuple-element.429), channel_id=1, source_target_pairs={{1,0},{2,1},{3,2},{4,3},{5,4},{6,5},{7,6},{8,7},{9,8},{10,9},{11,1... | collective-permute-start | bytes 2359304 | tf_op jit(solution)/shard_map/ppermute | solution.py:46
  302.2 37.4 %collective-permute-start.6 = (bf16[256,3072]{0,1:T(8,128)(2,1)S(1)}, bf16[256,3072]{0,1:T(8,128)(2,1)S(1)}, u32[]{:S(2)}, u32[]{:S(2)}) collective-permute-start(bf16[256,3072]{0,1:T(8,128)(2,1)S(1)} %pad_maximum_fusion), channel_id=1, source_target_pairs={{0,32},{32,64},{64,96},{96,128},{128,160},{160,192},{192,224},{224... | collective-permute-start | bytes 4718600 | tf_op jit(solution)/shard_map/ppermute | solution.py:77
  303.1 10.4 %collective-permute-start.9 = (bf16[128]{0:T(256)(128)(2,1)S(1)}, bf16[128]{0:T(256)(128)(2,1)S(1)}, u32[]{:S(2)}, u32[]{:S(2)}) collective-permute-start(bf16[128]{0:T(256)(128)(2,1)S(1)} %get-tuple-element.408), channel_id=1, source_target_pairs={{1,0},{2,1},{3,2},{4,3},{5,4},{6,5},{7,6},{8,7},{9,8},{10,9},{11,1... | collective-permute-start | bytes 776 | tf_op jit(solution)/shard_map/ppermute | solution.py:46
  311.6 29.7 %collective-permute-start.8 = (bf16[128,512]{1,0:T(8,128)(2,1)S(1)}, bf16[128,512]{1,0:T(8,128)(2,1)S(1)}, u32[]{:S(2)}, u32[]{:S(2)}) collective-permute-start(bf16[128,512]{1,0:T(8,128)(2,1)S(1)} %reduce_sum.32), channel_id=1, source_target_pairs={{1,0},{2,1},{3,2},{4,3},{5,4},{6,5},{7,6},{8,7},{9,8},{10,9},{11,1... | collective-permute-start | bytes 393224 | tf_op jit(solution)/shard_map/ppermute | solution.py:46
Sparse Core Ops, SparseCore 0:
  30.2 64.7 all-gather.2
where the time goes:
time: 351 us; the launch traced here: 349 us
  waiting for transfers between devices  105 us (30%)
  starting transfers between devices  92.2 us (26%)
  local copies, waits for them, and re-layouts  48.5 us (14%)
  other arithmetic  26.3 us (7%)
  blocking collectives  22.1 us (6%)
  loops' own time  21.5 us (6%)
  matrix products  17.3 us (5%)
  between operations  16.4 us (5%)
    ppermute x9, waiting for transfers between devices, passed_along(): return lax.ppermute(block, axis, route)  58.7 us
    all_to_all x1, starting transfers between devices, sent_and_summed(): tiles = lax.all_to_all(in_blocks(x, dim, devices), axis, 0, 0, tiled=True)  56.3 us
    ppermute x9, starting transfers between devices, passed_along(): return lax.ppermute(block, axis, route)  27.3 us
    ppermute x1, waiting for transfers between devices, from_behind(): lax.ppermute(x, axis, [(i, (i + by) % devices) for i in range(devices)])  25.4 us
    all_gather x1, blocking collectives, local(): lax.all_gather(for_sending(place_rows), 'ctx', axis=0, tiled=True)  22.1 us
    all_gather x1, waiting for transfers between devices, sent_together(): out = lax.all_gather(both, axis, axis=dim, tiled=True)  20.7 us
    while x4, local copies, waits for them, and re-layouts, local(): final_state = lax.scan(visit, start_state, stacked)[0]  14.9 us
    another operation x1, loops' own time, local(): final_state = lax.scan(visit, start_state, stacked)[0]  10.5 us
  transfers between devices with their start and end apart: 13, of which 5 were waited for; matrix products, arithmetic and copies ran while one was open for 18% of the time, Pallas kernels for 0%

commit v1 on v0

v1 whole, which is shorter than its diff:
```python
import math

import jax
import jax.numpy as jnp
from jax import lax
from jax.experimental import pallas as pl
from jax.experimental.pallas import tpu as pltpu
from jax.sharding import PartitionSpec as P

GROUPS = 4
WIDE = 6
D = 128
B = 128
COLS = WIDE * D
SECTIONS = 8
CTX = 32
TILE = 512
LOW = -1e30
SCALE = math.log2(math.e) / math.sqrt(D)
BF = jnp.bfloat16
F32 = jnp.float32
NCOPY = 260


def kernel(
    counts, q_in, k_in, v_in, ct_in, lg_in,
    handed, vgrad, ggrad,
    cb, qs, qr, cs, cr, ks, kr, vs, vr, ls, lr, gs, gr, fl, flr,
    kb, vb, sbuf, wbuf, qt, ot, dos, att_acc,
    pda, pdb, rba, rbb, ra, rb, ua, ub, ra2, rb2, dvf, dvr,
    br, hz, hr, csem, send_sems, recv_sems,
):
    sec = lax.axis_index("section")
    c = lax.axis_index("ctx")
    core = lax.rem(c, 2)
    y = lax.rem(lax.div(c, 2), 4)
    x = lax.div(c, 8)

    def dev(xx, yy, kk):
        return (sec, (lax.rem(xx + 8, 4) * 4 + lax.rem(yy + 8, 4)) * 2 + kk)

    nxt = (sec, lax.rem(c + 1, CTX))
    prv = (sec, lax.rem(c + CTX - 1, CTX))
    zup = (lax.rem(sec + 1, SECTIONS), c)
    zdn = (lax.rem(sec + SECTIONS - 1, SECTIONS), c)
    sib = (sec, c + 1 - 2 * core)
    MESH = pl.DeviceIdType.MESH

    made = []
    slots = {}

    def copy(name, src, dst, to):
        n = slots.setdefault(name, len(slots))
        made.append(
            pltpu.make_async_remote_copy(
                src_ref=src, dst_ref=dst, send_sem=send_sems.at[n], recv_sem=recv_sems.at[n],
                device_id=to, device_id_type=MESH,
            )
        )
        made[-1].start()
        return made[-1]

    def arrived(name, dst):
        n = slots[name]
        pltpu.make_async_remote_copy(
            src_ref=dst, dst_ref=dst, send_sem=send_sems.at[n], recv_sem=recv_sems.at[n],
            device_id=sib, device_id_type=MESH,
        ).wait_recv()

    bar = pltpu.get_barrier_semaphore()

    @pl.loop(1, CTX)
    def _(d):
        pl.semaphore_signal(bar, inc=1, device_id=(sec, lax.rem(c + d, CTX)), device_id_type=MESH)

    pl.semaphore_signal(bar, inc=1, device_id=zup, device_id_type=MESH)
    pl.semaphore_signal(bar, inc=1, device_id=zdn, device_id_type=MESH)

    held = counts[0, 0]
    two = held == 2
    cb[pl.ds(c, 1)] = jnp.full((1, 8, 128), held, jnp.int32)

    def pick(flag, a, b):
        return lax.select(jnp.broadcast_to(flag, a.shape), a, b)

    for g in range(GROUPS):
        kc = slice(g * D, (g + 1) * D)
        qc = slice(g * COLS, (g + 1) * COLS)
        ks[g] = pick(two, k_in[B:, kc], k_in[:B, kc])
        vs[g] = pick(two, v_in[B:, kc], v_in[:B, kc])
        qs[g] = pick(two, q_in[B:, qc], q_in[:B, qc])
        cs[g] = pick(two, ct_in[B:, qc], ct_in[:B, qc])
    lg = lg_in[...].astype(F32)
    ls[...] = jnp.broadcast_to(pick(two, lg[:, B:], lg[:, :B]), (8, 128))

    pl.semaphore_wait(bar, CTX + 1)

    @pl.loop(1, CTX)
    def _(d):
        pltpu.make_async_remote_copy(
            src_ref=cb.at[c], dst_ref=cb.at[c], send_sem=csem.at[0], recv_sem=csem.at[1],
            device_id=(sec, lax.rem(c + d, CTX)), device_id_type=MESH,
        ).start()

    copy("k", ks, kr, nxt)
    copy("v", vs, vr, nxt)
    copy("l", ls, lr, nxt)
    for g in range(GROUPS):
        copy(("q", g), qs.at[g], qr.at[g], nxt)
    for g in range(GROUPS):
        copy(("c", g), cs.at[g], cr.at[g], nxt)

    every = pltpu.make_async_remote_copy(
        src_ref=cb.at[pl.ds(0, CTX - 1)], dst_ref=cb.at[pl.ds(0, CTX - 1)],
        send_sem=csem.at[0], recv_sem=csem.at[1], device_id=sib, device_id_type=MESH,
    )
    every.wait_recv()
    order = lax.broadcasted_iota(jnp.int32, (CTX, 8, 128), 0)
    ahead = jnp.sum(jnp.where(order < c, cb[...] - 1, 0), axis=0).astype(F32)
    before = jnp.max(ahead)
    late = before > 0.5
    held_f = held.astype(F32)
    fl[0] = ahead
    fl[1] = jnp.full((8, 128), held_f, F32)

    arrived("k", kr)
    arrived("v", vr)
    for g in range(GROUPS):
        kc = slice(g * D, (g + 1) * D)
        kb[g, core, y, x] = pick(late, kr[g], k_in[:B, kc])
        vb[g, core, x, y] = pick(late, vr[g], v_in[:B, kc])
    copy("f", fl, flr, zup)

    def at(v):
        return lax.rem(v + 8, 4)

    for g in range(GROUPS):
        for d in (1, 3, 2):
            copy(("k1", g, d), kb.at[g, core, y, x], kb.at[g, core, y, x], dev(x + d, y, core))
            copy(("v1", g, d), vb.at[g, core, x, y], vb.at[g, core, x, y], dev(x, y + d, core))

    def gather_second(g):
        for d in (1, 3, 2):
            arrived(("k1", g, d), kb.at[g, core, y, at(x - d)])
            arrived(("v1", g, d), vb.at[g, core, x, at(y - d)])
        for d in (1, 3):
            copy(("k2", g, d), kb.at[g, core, y], kb.at[g, core, y], dev(x, y + d, core))
            copy(("v2", g, d), vb.at[g, core, x], vb.at[g, core, x], dev(x + d, y, core))
        copy(("kd", g, 0), kb.at[g, core, y], kb.at[g, core, y], sib)
        copy(("vd", g, 0), vb.at[g, core, x], vb.at[g, core, x], sib)

    def gather_third(g):
        for d in (1, 3):
            part = pl.ds(0, 2) if d == 1 else pl.ds(2, 2)
            yy, xx = at(y - d), at(x - d)
            arrived(("k2", g, d), kb.at[g, core, yy])
            copy(("k3", g, d), kb.at[g, core, yy, part], kb.at[g, core, yy, part], dev(x, y + d, core))
            arrived(("v2", g, d), vb.at[g, core, xx])
            copy(("v3", g, d), vb.at[g, core, xx, part], vb.at[g, core, xx, part], dev(x + d, y, core))
            copy(("kd", g, d), kb.at[g, core, yy], kb.at[g, core, yy], sib)
            copy(("vd", g, d), vb.at[g, core, xx], vb.at[g, core, xx], sib)

    def gather_fourth(g):
        yy, xx = at(y + 2), at(x + 2)
        for d in (1, 3):
            part = pl.ds(0, 2) if d == 1 else pl.ds(2, 2)
            arrived(("k3", g, d), kb.at[g, core, yy, part])
            arrived(("v3", g, d), vb.at[g, core, xx, part])
        copy(("kd", g, 2), kb.at[g, core, yy], kb.at[g, core, yy], sib)
        copy(("vd", g, 2), vb.at[g, core, xx], vb.at[g, core, xx], sib)

    def gather_last(g):
        for d in (0, 1, 3, 2):
            arrived(("kd", g, d), kb.at[g, 1 - core, at(y - d)])
            arrived(("vd", g, d), vb.at[g, 1 - core, at(x - d)])

    tiles = lax.div(c, 4) + 1
    lane = lax.broadcasted_iota(jnp.int32, (TILE, 2 * D), 1)
    gap = lax.broadcasted_iota(jnp.int32, (TILE, 2 * D), 0) - lax.rem(lane, D)

    def forward(g):
        arrived(("q", g), qr.at[g])
        qc = slice(g * COLS, (g + 1) * COLS)
        for h in range(WIDE):
            hc = slice(h * D, (h + 1) * D)
            full = pick(late, qr[g, :, hc], q_in[:B, g * COLS + h * D : g * COLS + (h + 1) * D])
            full = (full.astype(F32) * SCALE).T
            high = full.astype(BF)
            qt[:D, hc] = high
            qt[D:, hc] = (full - high.astype(F32)).astype(BF)

        def scores(j, tops):
            xx, y0 = lax.div(j, 2), lax.rem(j, 2) * 2
            one = jnp.concatenate(
                [kb[g, 0, y0, xx], kb[g, 1, y0, xx], kb[g, 0, y0 + 1, xx], kb[g, 1, y0 + 1, xx]], axis=0
            )
            both = jnp.concatenate([one, one], axis=1)
            bound = c * B - j * TILE
            out = []
            for p in range(3):
                pc = slice(p * 2 * D, (p + 1) * 2 * D)
                s = jnp.dot(both, qt[:, pc], preferred_element_type=F32)
                s = jnp.where(gap <= bound, s, LOW)
                sbuf[pl.ds(pl.multiple_of(j * TILE, TILE), TILE), pc] = s
                out.append(jnp.maximum(tops[p], jnp.max(s.reshape(TILE // 8, 8, 2 * D), axis=0)))
            return tuple(out)

        tops = lax.fori_loop(
            0, tiles, scores, tuple(jnp.full((8, 2 * D), LOW, F32) for _ in range(3))
        )
        tops = [jnp.max(t, axis=0, keepdims=True) for t in tops]
        ot[...] = jnp.zeros_like(ot)

        def weigh(j, _):
            xx, y0 = lax.div(j, 2), lax.rem(j, 2) * 2
            one = jnp.concatenate(
                [vb[g, 0, xx, y0], vb[g, 1, xx, y0], vb[g, 0, xx, y0 + 1], vb[g, 1, xx, y0 + 1]], axis=0
            )
            left = jnp.concatenate([one.T, jnp.ones((16, TILE), BF)], axis=0)
            rows = pl.ds(pl.multiple_of(j * TILE, TILE), TILE)
            for p in range(3):
                pc = slice(p * 2 * D, (p + 1) * 2 * D)
                w = jnp.exp2(sbuf[rows, pc] - tops[p]).astype(BF)
                wbuf[rows, pc] = w
                ot[:, pc] += jnp.dot(left, w, preferred_element_type=F32)
            return 0

        lax.fori_loop(0, tiles, weigh, 0)
        if g == 0:
            arrived("l", lr)
            gate_row = 1.0 / (1.0 + jnp.exp(-pick(late, lr[...], jnp.broadcast_to(lg[:, :B], (8, 128)))))
            gr[...] = gate_row
            att_acc[0] = jnp.broadcast_to(gate_row[:1], (B, D)).T
            att_acc[1] = jnp.zeros((B, D), F32)
        arrived(("c", g), cr.at[g])
        gate = att_acc[0]
        acc = att_acc[1]
        for h in range(WIDE):
            hc = slice(h * D, (h + 1) * D)
            inv = 1.0 / ot[D : D + 1, hc]
            attended = (ot[:D, hc] * inv).T
            br[g, :, hc] = (gate * attended).astype(BF)
            ct = pick(late, cr[g, :, hc], ct_in[:B, g * COLS + h * D : g * COLS + (h + 1) * D]).astype(F32)
            acc = acc + ct * attended
            dos[hc, :] = (gate * ct * jnp.broadcast_to(inv, (B, D)).T).astype(BF)
        att_acc[1] = acc
        copy(("h", g), br.at[g], hz.at[g], zup)

    def backward(g):
        def terms(j, _):
            xx, y0 = lax.div(j, 2), lax.rem(j, 2) * 2
            rows = pl.ds(pl.multiple_of(j * TILE, TILE), TILE)
            t = jnp.dot(wbuf[rows, :], dos[...], preferred_element_type=F32).astype(BF)
            for n in range(4):
                pda[g, n % 2, xx, y0 + n // 2] = t[n * B : n * B + 64]
                pdb[g, n % 2, y0 + n // 2, xx] = t[n * B + 64 : (n + 1) * B]
            return 0

        lax.fori_loop(0, tiles, terms, 0)

        def blank(j, _):
            xx, y0 = lax.div(j, 2), lax.rem(j, 2) * 2
            for n in range(4):
                pda[g, n % 2, xx, y0 + n // 2] = jnp.zeros((64, D), BF)
                pdb[g, n % 2, y0 + n // 2, xx] = jnp.zeros((64, D), BF)
            return 0

        lax.fori_loop(tiles, CTX // 4, blank, 0)
        copy(("a0", g), pda.at[g, 1 - core], rba.at[g], sib)
        copy(("b0", g), pdb.at[g, 1 - core], rbb.at[g], sib)

    def reduce_first(g):
        arrived(("a0", g), rba.at[g])
        arrived(("b0", g), rbb.at[g])
        rba[g] = (pda[g, core].astype(F32) + rba[g].astype(F32)).astype(BF)
        rbb[g] = (pdb[g, core].astype(F32) + rbb[g].astype(F32)).astype(BF)
        for d in (2, 1, 3):
            copy(("a1", g, d), rba.at[g, at(x + d)], ra.at[g, d - 1], dev(x + d, y, core))
            copy(("b1", g, d), rbb.at[g, at(y + d)], rb.at[g, d - 1], dev(x, y + d, core))

    def reduce_second(g):
        suma = rba[g, x].astype(F32)
        sumb = rbb[g, y].astype(F32)
        for d in (1, 3, 2):
            arrived(("a1", g, d), ra.at[g, d - 1])
            arrived(("b1", g, d), rb.at[g, d - 1])
            suma = suma + ra[g, d - 1].astype(F32)
            sumb = sumb + rb[g, d - 1].astype(F32)
        ua[g] = suma.astype(BF)
        ub[g] = sumb.astype(BF)
        for d in (2, 1, 3):
            copy(("a2", g, d), ua.at[g, at(y + d)], ra2.at[g, d - 1], dev(x, y + d, core))
            copy(("b2", g, d), ub.at[g, at(x + d)], rb2.at[g, d - 1], dev(x + d, y, core))

    def reduce_third(g):
        suma = ua[g, y].astype(F32)
        sumb = ub[g, x].astype(F32)
        for d in (1, 3, 2):
            arrived(("a2", g, d), ra2.at[g, d - 1])
            arrived(("b2", g, d), rb2.at[g, d - 1])
            suma = suma + ra2[g, d - 1].astype(F32)
            sumb = sumb + rb2[g, d - 1].astype(F32)
        dvf[g, :64] = suma.astype(BF)
        dvf[g, 64:] = sumb.astype(BF)
        copy(("r", g), dvf.at[g], dvr.at[g], prv)

    def slotted(first, held_n, mine, back):
        nothing = jnp.zeros_like(mine)
        carried = first + held_n > 1.5
        one = jnp.logical_and(carried, jnp.logical_and(held_n > 0.5, held_n < 1.5))
        both = jnp.logical_and(carried, held_n > 1.5)
        top = pick(first < 0.5, mine, pick(one, back, nothing))
        return top, pick(both, back, nothing)

    def grad_out(g):
        arrived(("r", g), dvr.at[g])
        kc = slice(g * D, (g + 1) * D)
        top, low = slotted(before, held_f, dvf[g], dvr[g])
        vgrad[:B, kc] = top
        vgrad[B:, kc] = low

    def hand_on(g):
        arrived(("h", g), hz.at[g])
        copy(("h2", g), hz.at[g], hr.at[g], prv)

    def hand_out(g):
        if g == 0:
            arrived("f", flr)
        arrived(("h2", g), hr.at[g])
        first, held_n = jnp.max(flr[0]), jnp.max(flr[1])
        for h in range(WIDE):
            hc = slice(h * D, (h + 1) * D)
            oc = slice(g * COLS + h * D, g * COLS + (h + 1) * D)
            top, low = slotted(first, held_n, hz[g, :, hc], hr[g, :, hc])
            handed[:B, oc] = top
            handed[B:, oc] = low

    def gate_out():
        gate_row = gr[...]
        total = jnp.sum(att_acc[1].T, axis=0, keepdims=True)
        ls_row = gate_row * (1.0 - gate_row) * jnp.broadcast_to(total, (8, 128))
        gs[0] = ls_row
        copy("g", gs.at[0], gs.at[1], prv)

    for g in range(GROUPS):
        gather_second(g)
    gather_third(0)
    gather_third(1)
    gather_fourth(0)
    gather_last(0)
    for g in range(GROUPS):
        forward(g)
        if g + 2 < GROUPS:
            gather_third(g + 2)
        if g + 1 < GROUPS:
            gather_fourth(g + 1)
        if g >= 1:
            reduce_second(g - 1)
            hand_on(g - 1)
        backward(g)
        if g == GROUPS - 1:
            gate_out()
        if g + 1 < GROUPS:
            gather_last(g + 1)
        reduce_first(g)
        if g >= 1:
            reduce_third(g - 1)
            hand_out(g - 1)
        if g >= 2:
            grad_out(g - 2)
    last = GROUPS - 1
    hand_on(last)
    reduce_second(last)
    grad_out(last - 1)
    hand_out(last)
    reduce_third(last)
    arrived("g", gs.at[1])
    top, low = slotted(before, held_f, gs[0, :1], gs[1, :1])
    ggrad[:, :B] = top.astype(BF)
    ggrad[:, B:] = low.astype(BF)
    grad_out(last)

    every.wait_send()
    for one in made:
        one.wait_send()


def local(queries, keys, values, cotangent, router_logits, positions, counts):
    del positions
    V = pl.BlockSpec(memory_space=pltpu.VMEM)
    G = GROUPS
    vm = pltpu.VMEM
    scratch = [
        vm((CTX, 8, 128), jnp.int32),
        vm((G, B, COLS), BF), vm((G, B, COLS), BF), vm((G, B, COLS), BF), vm((G, B, COLS), BF),
        vm((G, B, D), BF), vm((G, B, D), BF), vm((G, B, D), BF), vm((G, B, D), BF),
        vm((8, 128), F32), vm((8, 128), F32), vm((2, 8, 128), F32), vm((8, 128), F32),
        vm((2, 8, 128), F32), vm((2, 8, 128), F32),
        vm((G, 2, 4, 4, B, D), BF), vm((G, 2, 4, 4, B, D), BF),
        vm((CTX * B, COLS), F32), vm((CTX * B, COLS), BF),
        vm((2 * D, COLS), BF), vm((D + 16, COLS), F32), vm((COLS, D), BF), vm((2, B, D), F32),
        vm((G, 2, 4, 4, 64, D), BF), vm((G, 2, 4, 4, 64, D), BF),
        vm((G, 4, 4, 64, D), BF), vm((G, 4, 4, 64, D), BF),
        vm((G, 3, 4, 64, D), BF), vm((G, 3, 4, 64, D), BF),
        vm((G, 4, 64, D), BF), vm((G, 4, 64, D), BF),
        vm((G, 3, 64, D), BF), vm((G, 3, 64, D), BF),
        vm((G, B, D), BF), vm((G, B, D), BF),
        vm((G, B, COLS), BF), vm((G, B, COLS), BF), vm((G, B, COLS), BF),
        pltpu.SemaphoreType.DMA((2,)),
        pltpu.SemaphoreType.DMA((NCOPY,)),
        pltpu.SemaphoreType.DMA((NCOPY,)),
    ]
    handed, vgrad, ggrad = pl.pallas_call(
        kernel,
        out_shape=(
            jax.ShapeDtypeStruct((2 * B, G * COLS), BF),
            jax.ShapeDtypeStruct((2 * B, G * D), BF),
            jax.ShapeDtypeStruct((1, 2 * B), BF),
        ),
        in_specs=[pl.BlockSpec(memory_space=pltpu.SMEM)] + [V] * 5,
        out_specs=(V, V, V),
        scratch_shapes=scratch,
        compiler_params=pltpu.CompilerParams(
            collective_id=0, has_side_effects=True, vmem_limit_bytes=66_000_000
        ),
        name="routed_block",
    )(counts, queries[0], keys[0], values[0], cotangent[0], router_logits)
    return handed[None], vgrad[None], ggrad


def solution(mesh):
    return jax.shard_map(
        local,
        mesh=mesh,
        in_specs=(
            P("section", "ctx", None),
            P("section", "ctx", None),
            P("section", "ctx", None),
            P("section", "ctx", None),
            P("section", "ctx"),
            P("section", "ctx"),
            P("section", "ctx"),
        ),
        out_specs=(P("section", "ctx", None), P("section", "ctx", None), P("section", "ctx")),
        check_vma=False,
    )
```

time: 351 us -> 126 us (0.36)
  the two profiles are of different devices: /device:TPU:2 before, /device:TPU:1 now
where the time goes in v1:
time: 126 us
  Pallas kernels  121 us (96%)
  local copies, waits for them, and re-layouts  3.97 us (3%)
  between operations  1.3 us (1%)
    pallas_call x1, Pallas kernels, local(): pl.pallas_call(kernel, out_shape=(jax.ShapeDtypeStruct((2 * B, G * COLS),...  121 us
    unnamed x7, local copies, waits for them, and re-layouts  3.97 us

profile of v1, /device:TPU:1, one launch (start us, length us, event | category | flops | bytes accessed | tf_op | source)
XLA Modules:
  0.0 125.8 jit_solution(7342524028099532534)
XLA Ops:
  1.3 120.5 %routed_block.1 = (bf16[256,3072]{1,0:T(8,128)(2,1)}, bf16[256,512]{1,0:T(8,128)(2,1)}, bf16[1,256]{1,0:T(2,128)(2,1)}) custom-call(s32[1,1]{1,0:T(1,128)S(6)} %copy.12.counts, bf16[256,3072]{1,0:T(8,128)(2,1)} %bitcast.6, bf16[256,512]{1,0:T(8,128)(2,1)} %bitcast.9, bf16[256,512]{1,0:T(8,128)(2,1)} %bitcast.10, bf16[256,3072]{1,0:T(8,128)(2,1)} %bitcast.7, ...), custom_call_target="tpu_custom_call" | custom-call | tf_op jit(solution)/shard_map/routed_block/pallas_call | solution.py:413
  121.8 0.0 copy-start
  121.8 0.0 copy-start.1
  121.8 2.7 %copy.13 = bf16[1,256,3072]{2,1,0:T(8,128)(2,1)} copy(bf16[1,256,3072]{2,1,0:T(8,128)(2,1)} %bitcast.8) | data formatting | bytes 3145728
  124.5 0.0 copy-done
  124.5 0.7 copy.14
  125.2 0.0 copy-done.1
  125.2 0.6 copy.15
Async XLA Ops:
  121.8 2.7 %copy-start = (bf16[256,512]{1,0:T(8,128)(2,1)S(1)}, bf16[256,512]{1,0:T(8,128)(2,1)}, u32[]{:S(2)}) copy-start(bf16[256,512]{1,0:T(8,128)(2,1)} %get-tuple-element.7) | copy-start | bytes 786436
  121.8 3.4 %copy-start.1 = (bf16[1,256]{1,0:T(2,128)(2,1)S(1)}, bf16[1,256]{1,0:T(2,128)(2,1)}, u32[]{:S(2)}) copy-start(bf16[1,256]{1,0:T(2,128)(2,1)} %get-tuple-element.14) | copy-start | bytes 1540

commit v2 on v1

--- a/solution.py
+++ b/solution.py
@@ -20,15 +20,17 @@
 BF = jnp.bfloat16
 F32 = jnp.float32
 NCOPY = 260
+DIRECT = False
+Y_LARGE = (0, 1, 2, 3)
 
 
 def kernel(
     counts, q_in, k_in, v_in, ct_in, lg_in,
-    handed, vgrad, ggrad,
-    cb, qs, qr, cs, cr, ks, kr, vs, vr, ls, lr, gs, gr, fl, flr,
+    hz, hr, dvf, dvr, gs, fl, flr,
+    cb, qs, qr, cs, cr, ks, kr, vs, vr, ls, lr, gr,
     kb, vb, sbuf, wbuf, qt, ot, dos, att_acc,
-    pda, pdb, rba, rbb, ra, rb, ua, ub, ra2, rb2, dvf, dvr,
-    br, hz, hr, csem, send_sems, recv_sems,
+    pda, pdb, rba, rbb, ra, rb, ua, ub, ra2, rb2,
+    br, csem, send_sems, recv_sems,
 ):
     sec = lax.axis_index("section")
     c = lax.axis_index("ctx")
@@ -78,7 +80,7 @@
 
     held = counts[0, 0]
     two = held == 2
-    cb[pl.ds(c, 1)] = jnp.full((1, 8, 128), held, jnp.int32)
+    cb[pl.ds(c, 1)] = jnp.full((1, 1, 128), held, jnp.int32)
 
     def pick(flag, a, b):
         return lax.select(jnp.broadcast_to(flag, a.shape), a, b)
@@ -105,80 +107,110 @@
     copy("k", ks, kr, nxt)
     copy("v", vs, vr, nxt)
     copy("l", ls, lr, nxt)
-    for g in range(GROUPS):
-        copy(("q", g), qs.at[g], qr.at[g], nxt)
-    for g in range(GROUPS):
-        copy(("c", g), cs.at[g], cr.at[g], nxt)
 
     every = pltpu.make_async_remote_copy(
         src_ref=cb.at[pl.ds(0, CTX - 1)], dst_ref=cb.at[pl.ds(0, CTX - 1)],
         send_sem=csem.at[0], recv_sem=csem.at[1], device_id=sib, device_id_type=MESH,
     )
     every.wait_recv()
-    order = lax.broadcasted_iota(jnp.int32, (CTX, 8, 128), 0)
+    order = lax.broadcasted_iota(jnp.int32, (CTX, 1, 128), 0)
     ahead = jnp.sum(jnp.where(order < c, cb[...] - 1, 0), axis=0).astype(F32)
     before = jnp.max(ahead)
     late = before > 0.5
     held_f = held.astype(F32)
-    fl[0] = ahead
+    fl[0] = jnp.broadcast_to(ahead, (8, 128))
     fl[1] = jnp.full((8, 128), held_f, F32)
 
     arrived("k", kr)
     arrived("v", vr)
+
+    def at(v):
+        return lax.rem(v + 8, 4)
+
+    parts = {
+        (kind, g): (kb if kind == "k" else vb, kind == "k" and g in Y_LARGE)
+        for kind in ("k", "v")
+        for g in range(GROUPS)
+    }
+
+    def place(kind, g):
+        buf, y_large = parts[kind, g]
+        small = (lambda d: dev(x + d, y, core)) if y_large else (lambda d: dev(x, y + d, core))
+        large = (lambda d: dev(x, y + d, core)) if y_large else (lambda d: dev(x + d, y, core))
+        return buf, y_large, (y, x) if y_large else (x, y), small, large
+
+    def block(kind, g, kk, xx, yy):
+        buf, y_large = parts[kind, g]
+        return buf[g, kk, yy, xx] if y_large else buf[g, kk, xx, yy]
+
     for g in range(GROUPS):
         kc = slice(g * D, (g + 1) * D)
-        kb[g, core, y, x] = pick(late, kr[g], k_in[:B, kc])
-        vb[g, core, x, y] = pick(late, vr[g], v_in[:B, kc])
+        for kind, got, own in (("k", kr, k_in), ("v", vr, v_in)):
+            buf, _, (a, b), _, _ = place(kind, g)
+            buf[g, core, a, b] = pick(late, got[g], own[:B, kc])
     copy("f", fl, flr, zup)
 
-    def at(v):
-        return lax.rem(v + 8, 4)
-
-    for g in range(GROUPS):
-        for d in (1, 3, 2):
-            copy(("k1", g, d), kb.at[g, core, y, x], kb.at[g, core, y, x], dev(x + d, y, core))
-            copy(("v1", g, d), vb.at[g, core, x, y], vb.at[g, core, x, y], dev(x, y + d, core))
+    def pass_on2(g):
+        pass_on("q", g)
+        pass_on("c", g)
+
+    def gather_one(g):
+        for kind in ("k", "v"):
+            buf, _, (a, b), small, _ = place(kind, g)
+            own = buf.at[g, core, a, b]
+            for d in (1, 3, 2):
+                copy((kind, 1, g, d), own, own, small(d))
 
     def gather_second(g):
-        for d in (1, 3, 2):
-            arrived(("k1", g, d), kb.at[g, core, y, at(x - d)])
-            arrived(("v1", g, d), vb.at[g, core, x, at(y - d)])
-        for d in (1, 3):
-            copy(("k2", g, d), kb.at[g, core, y], kb.at[g, core, y], dev(x, y + d, core))
-            copy(("v2", g, d), vb.at[g, core, x], vb.at[g, core, x], dev(x + d, y, core))
-        copy(("kd", g, 0), kb.at[g, core, y], kb.at[g, core, y], sib)
-        copy(("vd", g, 0), vb.at[g, core, x], vb.at[g, core, x], sib)
+        for kind in ("k", "v"):
+            buf, _, (a, b), _, large = place(kind, g)
+            for d in (1, 3, 2):
+                arrived((kind, 1, g, d), buf.at[g, core, a, at(b - d)])
+            own = buf.at[g, core, a]
+            for d in (1, 3, 2) if DIRECT else (1, 3):
+                copy((kind, 2, g, d), own, own, large(d))
+            copy((kind, 4, g, 0), own, own, sib)
 
     def gather_third(g):
         for d in (1, 3):
-            part = pl.ds(0, 2) if d == 1 else pl.ds(2, 2)
-            yy, xx = at(y - d), at(x - d)
-            arrived(("k2", g, d), kb.at[g, core, yy])
-            copy(("k3", g, d), kb.at[g, core, yy, part], kb.at[g, core, yy, part], dev(x, y + d, core))
-            arrived(("v2", g, d), vb.at[g, core, xx])
-            copy(("v3", g, d), vb.at[g, core, xx, part], vb.at[g, core, xx, part], dev(x + d, y, core))
-            copy(("kd", g, d), kb.at[g, core, yy], kb.at[g, core, yy], sib)
-            copy(("vd", g, d), vb.at[g, core, xx], vb.at[g, core, xx], sib)
+            for kind in ("k", "v"):
+                buf, _, (a, b), _, large = place(kind, g)
+                aa = at(a - d)
+                came = buf.at[g, core, aa]
+                arrived((kind, 2, g, d), came)
+                if not DIRECT:
+                    half = buf.at[g, core, aa, pl.ds(d - 1, 2)]
+                    copy((kind, 3, g, d), half, half, large(d))
+                copy((kind, 4, g, d), came, came, sib)
 
     def gather_fourth(g):
-        yy, xx = at(y + 2), at(x + 2)
-        for d in (1, 3):
-            part = pl.ds(0, 2) if d == 1 else pl.ds(2, 2)
-            arrived(("k3", g, d), kb.at[g, core, yy, part])
-            arrived(("v3", g, d), vb.at[g, core, xx, part])
-        copy(("kd", g, 2), kb.at[g, core, yy], kb.at[g, core, yy], sib)
-        copy(("vd", g, 2), vb.at[g, core, xx], vb.at[g, core, xx], sib)
+        for kind in ("k", "v"):
+            buf, _, (a, b), _, _ = place(kind, g)
+            aa = at(a + 2)
+            if DIRECT:
+                arrived((kind, 2, g, 2), buf.at[g, core, aa])
+            else:
+                for d in (1, 3):
+                    arrived((kind, 3, g, d), buf.at[g, core, aa, pl.ds(d - 1, 2)])
+            copy((kind, 4, g, 2), buf.at[g, core, aa], buf.at[g, core, aa], sib)
 
     def gather_last(g):
-        for d in (0, 1, 3, 2):
-            arrived(("kd", g, d), kb.at[g, 1 - core, at(y - d)])
-            arrived(("vd", g, d), vb.at[g, 1 - core, at(x - d)])
+        for kind in ("k", "v"):
+            buf, _, (a, b), _, _ = place(kind, g)
+            for d in (0, 1, 3, 2):
+                arrived((kind, 4, g, d), buf.at[g, 1 - core, at(a - d)])
+
+    def pass_on(name, g):
+        if name == "q":
+            copy(("q", g), qs.at[g], qr.at[g], nxt)
+        else:
+            copy(("c", g), cs.at[g], cr.at[g], nxt)
 
     tiles = lax.div(c, 4) + 1
     lane = lax.broadcasted_iota(jnp.int32, (TILE, 2 * D), 1)
     gap = lax.broadcasted_iota(jnp.int32, (TILE, 2 * D), 0) - lax.rem(lane, D)
 
-    def forward(g):
+    def forward(g, between, after):
         arrived(("q", g), qr.at[g])
         qc = slice(g * COLS, (g + 1) * COLS)
         for h in range(WIDE):
@@ -192,7 +224,7 @@
         def scores(j, tops):
             xx, y0 = lax.div(j, 2), lax.rem(j, 2) * 2
             one = jnp.concatenate(
-                [kb[g, 0, y0, xx], kb[g, 1, y0, xx], kb[g, 0, y0 + 1, xx], kb[g, 1, y0 + 1, xx]], axis=0
+                [block("k", g, n % 2, xx, y0 + n // 2) for n in range(4)], axis=0
             )
             both = jnp.concatenate([one, one], axis=1)
             bound = c * B - j * TILE
@@ -210,11 +242,12 @@
         )
         tops = [jnp.max(t, axis=0, keepdims=True) for t in tops]
         ot[...] = jnp.zeros_like(ot)
+        between()
 
         def weigh(j, _):
             xx, y0 = lax.div(j, 2), lax.rem(j, 2) * 2
             one = jnp.concatenate(
-                [vb[g, 0, xx, y0], vb[g, 1, xx, y0], vb[g, 0, xx, y0 + 1], vb[g, 1, xx, y0 + 1]], axis=0
+                [block("v", g, n % 2, xx, y0 + n // 2) for n in range(4)], axis=0
             )
             left = jnp.concatenate([one.T, jnp.ones((16, TILE), BF)], axis=0)
             rows = pl.ds(pl.multiple_of(j * TILE, TILE), TILE)
@@ -226,6 +259,7 @@
             return 0
 
         lax.fori_loop(0, tiles, weigh, 0)
+        after()
         if g == 0:
             arrived("l", lr)
             gate_row = 1.0 / (1.0 + jnp.exp(-pick(late, lr[...], jnp.broadcast_to(lg[:, :B], (8, 128)))))
@@ -244,7 +278,7 @@
             acc = acc + ct * attended
             dos[hc, :] = (gate * ct * jnp.broadcast_to(inv, (B, D)).T).astype(BF)
         att_acc[1] = acc
-        copy(("h", g), br.at[g], hz.at[g], zup)
+        copy(("h", g), br.at[g], hz.at[:, g * COLS : (g + 1) * COLS], zup)
 
     def backward(g):
         def terms(j, _):
@@ -300,40 +334,15 @@
             arrived(("b2", g, d), rb2.at[g, d - 1])
             suma = suma + ra2[g, d - 1].astype(F32)
             sumb = sumb + rb2[g, d - 1].astype(F32)
-        dvf[g, :64] = suma.astype(BF)
-        dvf[g, 64:] = sumb.astype(BF)
-        copy(("r", g), dvf.at[g], dvr.at[g], prv)
-
-    def slotted(first, held_n, mine, back):
-        nothing = jnp.zeros_like(mine)
-        carried = first + held_n > 1.5
-        one = jnp.logical_and(carried, jnp.logical_and(held_n > 0.5, held_n < 1.5))
-        both = jnp.logical_and(carried, held_n > 1.5)
-        top = pick(first < 0.5, mine, pick(one, back, nothing))
-        return top, pick(both, back, nothing)
-
-    def grad_out(g):
-        arrived(("r", g), dvr.at[g])
         kc = slice(g * D, (g + 1) * D)
-        top, low = slotted(before, held_f, dvf[g], dvr[g])
-        vgrad[:B, kc] = top
-        vgrad[B:, kc] = low
+        dvf[:64, kc] = suma.astype(BF)
+        dvf[64:, kc] = sumb.astype(BF)
+        copy(("r", g), dvf.at[:, kc], dvr.at[:, kc], prv)
 
     def hand_on(g):
-        arrived(("h", g), hz.at[g])
-        copy(("h2", g), hz.at[g], hr.at[g], prv)
-
-    def hand_out(g):
-        if g == 0:
-            arrived("f", flr)
-        arrived(("h2", g), hr.at[g])
-        first, held_n = jnp.max(flr[0]), jnp.max(flr[1])
-        for h in range(WIDE):
-            hc = slice(h * D, (h + 1) * D)
-            oc = slice(g * COLS + h * D, g * COLS + (h + 1) * D)
-            top, low = slotted(first, held_n, hz[g, :, hc], hr[g, :, hc])
-            handed[:B, oc] = top
-            handed[B:, oc] = low
+        oc = slice(g * COLS, (g + 1) * COLS)
+        arrived(("h", g), hz.at[:, oc])
+        copy(("h2", g), hz.at[:, oc], hr.at[:, oc], prv)
 
     def gate_out():
         gate_row = gr[...]
@@ -343,46 +352,96 @@
         copy("g", gs.at[0], gs.at[1], prv)
 
     for g in range(GROUPS):
-        gather_second(g)
+        gather_one(g)
+    pass_on("q", 0)
+    gather_second(0)
+    gather_second(1)
+    pass_on("c", 0)
     gather_third(0)
+    gather_second(2)
+    gather_fourth(0)
+    gather_second(3)
+    pass_on("q", 1)
     gather_third(1)
-    gather_fourth(0)
     gather_last(0)
+    pass_on("c", 1)
+    plan = {
+        (0, 0): [(pass_on2, 2), (gather_third, 2)],
+        (0, 1): [(gather_fourth, 1)],
+        (0, 2): [(gather_third, 3), (pass_on2, 3)],
+        (0, 3): [(gather_last, 1), (gather_fourth, 2)],
+        (1, 0): [(reduce_first, 0)],
+        (1, 1): [(hand_on, 0), (gather_fourth, 3)],
+        (1, 2): [(gather_last, 2)],
+        (1, 3): [(reduce_second, 0)],
+        (2, 0): [(reduce_first, 1)],
+        (2, 1): [(reduce_third, 0), (hand_on, 1)],
+        (2, 2): [(gather_last, 3)],
+        (2, 3): [(reduce_second, 1)],
+        (3, 0): [(reduce_first, 2)],
+        (3, 1): [(reduce_third, 1), (hand_on, 2)],
+        (3, 2): [(reduce_second, 2)],
+        (3, 3): [],
+    }
     for g in range(GROUPS):
-        forward(g)
-        if g + 2 < GROUPS:
-            gather_third(g + 2)
-        if g + 1 < GROUPS:
-            gather_fourth(g + 1)
-        if g >= 1:
-            reduce_second(g - 1)
-            hand_on(g - 1)
+        def at_slot(n):
+            for what, k in plan[g, n]:
+                what(k)
+
+        forward(g, lambda: at_slot(0), lambda: at_slot(1))
+        at_slot(2)
         backward(g)
         if g == GROUPS - 1:
             gate_out()
-        if g + 1 < GROUPS:
-            gather_last(g + 1)
-        reduce_first(g)
-        if g >= 1:
-            reduce_third(g - 1)
-            hand_out(g - 1)
-        if g >= 2:
-            grad_out(g - 2)
+        at_slot(3)
     last = GROUPS - 1
+    reduce_first(last)
+    reduce_third(2)
+    reduce_second(last)
     hand_on(last)
-    reduce_second(last)
-    grad_out(last - 1)
-    hand_out(last)
     reduce_third(last)
+    arrived("f", flr)
     arrived("g", gs.at[1])
-    top, low = slotted(before, held_f, gs[0, :1], gs[1, :1])
-    ggrad[:, :B] = top.astype(BF)
-    ggrad[:, B:] = low.astype(BF)
-    grad_out(last)
+    for g in range(GROUPS):
+        arrived(("h2", g), hr.at[:, g * COLS : (g + 1) * COLS])
+        arrived(("r", g), dvr.at[:, g * D : (g + 1) * D])
 
     every.wait_send()
     for one in made:
         one.wait_send()
+
+
+def finish(hz, hr, dvf, dvr, gs, fl, flr, handed, vgrad, ggrad):
+    def slotted(flags, mine, back, out, cols):
+        first, held = jnp.max(flags[0]), jnp.max(flags[1])
+        carried = first + held > 1.5
+        one = jnp.logical_and(carried, jnp.logical_and(held > 0.5, held < 1.5))
+        both = jnp.logical_and(carried, held > 1.5)
+        nothing = jnp.zeros_like(mine)
+
+        def pick(flag, a, b):
+            return lax.select(jnp.broadcast_to(flag, a.shape), a, b)
+
+        out(pick(first < 0.5, mine, pick(one, back, nothing)), pick(both, back, nothing), cols)
+
+    def rows(ref):
+        def put(top, low, cols):
+            ref[:B, cols] = top
+            ref[B:, cols] = low
+
+        return put
+
+    def lanes(top, low, cols):
+        ggrad[:, :B] = top.astype(BF)
+        ggrad[:, B:] = low.astype(BF)
+
+    for n in range(GROUPS * WIDE):
+        cols = slice(n * D, (n + 1) * D)
+        slotted(flr, hz[:, cols], hr[:, cols], rows(handed), cols)
+    for n in range(GROUPS):
+        cols = slice(n * D, (n + 1) * D)
+        slotted(fl, dvf[:, cols], dvr[:, cols], rows(vgrad), cols)
+    slotted(fl, gs[0, :1], gs[1, :1], lanes, None)
 
 
 def local(queries, keys, values, cotangent, router_logits, positions, counts):
@@ -391,11 +450,10 @@
     G = GROUPS
     vm = pltpu.VMEM
     scratch = [
-        vm((CTX, 8, 128), jnp.int32),
+        vm((CTX, 1, 128), jnp.int32),
         vm((G, B, COLS), BF), vm((G, B, COLS), BF), vm((G, B, COLS), BF), vm((G, B, COLS), BF),
         vm((G, B, D), BF), vm((G, B, D), BF), vm((G, B, D), BF), vm((G, B, D), BF),
-        vm((8, 128), F32), vm((8, 128), F32), vm((2, 8, 128), F32), vm((8, 128), F32),
-        vm((2, 8, 128), F32), vm((2, 8, 128), F32),
+        vm((8, 128), F32), vm((8, 128), F32), vm((8, 128), F32),
         vm((G, 2, 4, 4, B, D), BF), vm((G, 2, 4, 4, B, D), BF),
         vm((CTX * B, COLS), F32), vm((CTX * B, COLS), BF),
         vm((2 * D, COLS), BF), vm((D + 16, COLS), F32), vm((COLS, D), BF), vm((2, B, D), F32),
@@ -404,27 +462,41 @@
         vm((G, 3, 4, 64, D), BF), vm((G, 3, 4, 64, D), BF),
         vm((G, 4, 64, D), BF), vm((G, 4, 64, D), BF),
         vm((G, 3, 64, D), BF), vm((G, 3, 64, D), BF),
-        vm((G, B, D), BF), vm((G, B, D), BF),
-        vm((G, B, COLS), BF), vm((G, B, COLS), BF), vm((G, B, COLS), BF),
+        vm((G, B, COLS), BF),
         pltpu.SemaphoreType.DMA((2,)),
         pltpu.SemaphoreType.DMA((NCOPY,)),
         pltpu.SemaphoreType.DMA((NCOPY,)),
     ]
-    handed, vgrad, ggrad = pl.pallas_call(
+    hz, hr, dvf, dvr, gs, fl, flr = pl.pallas_call(
         kernel,
         out_shape=(
-            jax.ShapeDtypeStruct((2 * B, G * COLS), BF),
-            jax.ShapeDtypeStruct((2 * B, G * D), BF),
-            jax.ShapeDtypeStruct((1, 2 * B), BF),
+            jax.ShapeDtypeStruct((B, G * COLS), BF),
+            jax.ShapeDtypeStruct((B, G * COLS), BF),
+            jax.ShapeDtypeStruct((B, G * D), BF),
+            jax.ShapeDtypeStruct((B, G * D), BF),
+            jax.ShapeDtypeStruct((2, 8, 128), F32),
+            jax.ShapeDtypeStruct((2, 8, 128), F32),
+            jax.ShapeDtypeStruct((2, 8, 128), F32),
         ),
         in_specs=[pl.BlockSpec(memory_space=pltpu.SMEM)] + [V] * 5,
-        out_specs=(V, V, V),
+        out_specs=(V,) * 7,
         scratch_shapes=scratch,
         compiler_params=pltpu.CompilerParams(
             collective_id=0, has_side_effects=True, vmem_limit_bytes=66_000_000
         ),
         name="routed_block",
     )(counts, queries[0], keys[0], values[0], cotangent[0], router_logits)
+    handed, vgrad, ggrad = pl.pallas_call(
+        finish,
+        out_shape=(
+            jax.ShapeDtypeStruct((2 * B, G * COLS), BF),
+            jax.ShapeDtypeStruct((2 * B, G * D), BF),
+            jax.ShapeDtypeStruct((1, 2 * B), BF),
+        ),
+        in_specs=[V] * 7,
+        out_specs=(V, V, V),
+        name="slots",
+    )(hz, hr, dvf, dvr, gs, fl, flr)
     return handed[None], vgrad[None], ggrad
 
 

time: 126 us -> 108 us (0.86)
  Pallas kernels: 121 us -> 106 us
  local copies, waits for them, and re-layouts: 3.97 us -> 0 us
    pallas_call x1 -> x2, Pallas kernels: 121 us -> 106 us  [the longest x1 103 us: local(): pl.pallas_call(kernel, out_shape=(jax.ShapeDtypeStruct((B, G * COLS), BF)...]
    unnamed x7 -> x0, local copies, waits for them, and re-layouts: 3.97 us -> none
where the time goes in v2:
time: 108 us
  Pallas kernels  106 us (98%)
  between operations  1.29 us (1%)
    pallas_call x1, Pallas kernels, local(): pl.pallas_call(kernel, out_shape=(jax.ShapeDtypeStruct((B, G * COLS), BF)...  103 us
    pallas_call x1, Pallas kernels, local(): pl.pallas_call(finish, out_shape=(jax.ShapeDtypeStruct((2 * B, G * COLS),...  3.32 us

profile of v2, /device:TPU:1, one launch (start us, length us, event | category | flops | bytes accessed | tf_op | source)
XLA Modules:
  0.0 107.7 jit_solution(1085225302973769750)
XLA Ops:
  1.3 103.1 %routed_block.1 = (bf16[128,3072]{1,0:T(8,128)(2,1)}, bf16[128,3072]{1,0:T(8,128)(2,1)}, bf16[128,512]{1,0:T(8,128)(2,1)}, bf16[128,512]{1,0:T(8,128)(2,1)}, f32...) custom-call(s32[1,1]{1,0:T(1,128)S(6)} %copy.9.counts, bf16[256,3072]{1,0:T(8,128)(2,1)} %bitcast.6, ...), custom_call_target="tpu_custom_call" | custom-call | tf_op jit(solution)/shard_map/routed_block/pallas_call | solution.py:470
  104.4 3.3 %slots.1 = (bf16[256,3072]{1,0:T(8,128)(2,1)}, bf16[256,512]{1,0:T(8,128)(2,1)}, bf16[1,256]{1,0:T(2,128)(2,1)}) custom-call(bf16[128,3072]{1,0:T(8,128)(2,1)} %get-tuple-element.13.hz, bf16[128,3072]{1,0:T(8,128)(2,1)} %get-tuple-element.14.hr, bf16[128,512]{1,0:T(8,128)(2,1)} %get-tuple-element.15.dvf, bf16[128,512]{1,0:T(8,128)(2,1)} %get-tuple-element.16.dvr, ...), custom_call_target="tpu_custom_call" | custom-call | tf_op jit(solution)/shard_map/slots/pallas_call | solution.py:489

commit v3 on v2

--- a/solution.py
+++ b/solution.py
@@ -14,13 +14,14 @@
 COLS = WIDE * D
 SECTIONS = 8
 CTX = 32
-TILE = 512
+TILE = 2048
+NB = TILE // B
 LOW = -1e30
 SCALE = math.log2(math.e) / math.sqrt(D)
 BF = jnp.bfloat16
 F32 = jnp.float32
-NCOPY = 260
-DIRECT = False
+NCOPY = 57
+DIRECT = (0,)
 Y_LARGE = (0, 1, 2, 3)
 
 
@@ -48,26 +49,33 @@
     sib = (sec, c + 1 - 2 * core)
     MESH = pl.DeviceIdType.MESH
 
-    made = []
+    sets = {
+        "s1": kb.at[0, 0, pl.ds(0, 2), pl.ds(0, 3)],
+        "s2": kb.at[0, 0, pl.ds(0, 2)],
+        "s3": kb.at[0, 0, pl.ds(0, 2)],
+        "s4": kb.at[0],
+        "a0": pda.at[0],
+        "a1": pda.at[0, pl.ds(0, 2), pl.ds(0, 3)],
+        "a3": pda.at[0, 0, pl.ds(0, 2), pl.ds(0, 3)],
+    }
     slots = {}
 
     def copy(name, src, dst, to):
-        n = slots.setdefault(name, len(slots))
-        made.append(
-            pltpu.make_async_remote_copy(
-                src_ref=src, dst_ref=dst, send_sem=send_sems.at[n], recv_sem=recv_sems.at[n],
-                device_id=to, device_id_type=MESH,
-            )
+        n, _ = slots.setdefault(name, (len(slots), sets.get(name[0], dst)))
+        pltpu.make_async_remote_copy(
+            src_ref=src, dst_ref=dst, send_sem=send_sems.at[n], recv_sem=recv_sems.at[n],
+            device_id=to, device_id_type=MESH,
+        ).start()
+
+    def whole(name):
+        n, ref = slots[name]
+        return pltpu.make_async_remote_copy(
+            src_ref=ref, dst_ref=ref, send_sem=send_sems.at[n], recv_sem=recv_sems.at[n],
+            device_id=sib, device_id_type=MESH,
         )
-        made[-1].start()
-        return made[-1]
-
-    def arrived(name, dst):
-        n = slots[name]
-        pltpu.make_async_remote_copy(
-            src_ref=dst, dst_ref=dst, send_sem=send_sems.at[n], recv_sem=recv_sems.at[n],
-            device_id=sib, device_id_type=MESH,
-        ).wait_recv()
+
+    def arrived(*name):
+        whole(name).wait_recv()
 
     bar = pltpu.get_barrier_semaphore()
 
@@ -104,9 +112,10 @@
             device_id=(sec, lax.rem(c + d, CTX)), device_id_type=MESH,
         ).start()
 
-    copy("k", ks, kr, nxt)
-    copy("v", vs, vr, nxt)
-    copy("l", ls, lr, nxt)
+    copy(("k",), ks, kr, nxt)
+    copy(("v",), vs, vr, nxt)
+    copy(("l",), ls, lr, nxt)
+    copy(("q", 0), qs.at[0], qr.at[0], nxt)
 
     every = pltpu.make_async_remote_copy(
         src_ref=cb.at[pl.ds(0, CTX - 1)], dst_ref=cb.at[pl.ds(0, CTX - 1)],
@@ -121,8 +130,8 @@
     fl[0] = jnp.broadcast_to(ahead, (8, 128))
     fl[1] = jnp.full((8, 128), held_f, F32)
 
-    arrived("k", kr)
-    arrived("v", vr)
+    arrived("k")
+    arrived("v")
 
     def at(v):
         return lax.rem(v + 8, 4)
@@ -148,10 +157,12 @@
         for kind, got, own in (("k", kr, k_in), ("v", vr, v_in)):
             buf, _, (a, b), _, _ = place(kind, g)
             buf[g, core, a, b] = pick(late, got[g], own[:B, kc])
-    copy("f", fl, flr, zup)
-
-    def pass_on2(g):
+    copy(("f",), fl, flr, zup)
+
+    def pass_q(g):
         pass_on("q", g)
+
+    def pass_c(g):
         pass_on("c", g)
 
     def gather_one(g):
@@ -159,46 +170,43 @@
             buf, _, (a, b), small, _ = place(kind, g)
             own = buf.at[g, core, a, b]
             for d in (1, 3, 2):
-                copy((kind, 1, g, d), own, own, small(d))
+                copy(("s1", g), own, own, small(d))
 
     def gather_second(g):
+        arrived("s1", g)
+        for d in (1, 3, 2) if g in DIRECT else (1, 3):
+            for kind in ("k", "v"):
+                buf, _, (a, b), _, large = place(kind, g)
+                own = buf.at[g, core, a]
+                copy(("s2", g, d), own, own, large(d))
         for kind in ("k", "v"):
-            buf, _, (a, b), _, large = place(kind, g)
-            for d in (1, 3, 2):
-                arrived((kind, 1, g, d), buf.at[g, core, a, at(b - d)])
-            own = buf.at[g, core, a]
-            for d in (1, 3, 2) if DIRECT else (1, 3):
-                copy((kind, 2, g, d), own, own, large(d))
-            copy((kind, 4, g, 0), own, own, sib)
+            buf, _, (a, b), _, _ = place(kind, g)
+            copy(("s4", g), buf.at[g, core, a], buf.at[g, core, a], sib)
 
     def gather_third(g):
         for d in (1, 3):
+            arrived("s2", g, d)
             for kind in ("k", "v"):
                 buf, _, (a, b), _, large = place(kind, g)
                 aa = at(a - d)
                 came = buf.at[g, core, aa]
-                arrived((kind, 2, g, d), came)
-                if not DIRECT:
+                if g not in DIRECT:
                     half = buf.at[g, core, aa, pl.ds(d - 1, 2)]
-                    copy((kind, 3, g, d), half, half, large(d))
-                copy((kind, 4, g, d), came, came, sib)
+                    copy(("s3", g), half, half, large(d))
+                copy(("s4", g), came, came, sib)
 
     def gather_fourth(g):
+        if g in DIRECT:
+            arrived("s2", g, 2)
+        else:
+            arrived("s3", g)
         for kind in ("k", "v"):
             buf, _, (a, b), _, _ = place(kind, g)
             aa = at(a + 2)
-            if DIRECT:
-                arrived((kind, 2, g, 2), buf.at[g, core, aa])
-            else:
-                for d in (1, 3):
-                    arrived((kind, 3, g, d), buf.at[g, core, aa, pl.ds(d - 1, 2)])
-            copy((kind, 4, g, 2), buf.at[g, core, aa], buf.at[g, core, aa], sib)
+            copy(("s4", g), buf.at[g, core, aa], buf.at[g, core, aa], sib)
 
     def gather_last(g):
-        for kind in ("k", "v"):
-            buf, _, (a, b), _, _ = place(kind, g)
-            for d in (0, 1, 3, 2):
-                arrived((kind, 4, g, d), buf.at[g, 1 - core, at(a - d)])
+        arrived("s4", g)
 
     def pass_on(name, g):
         if name == "q":
@@ -206,12 +214,12 @@
         else:
             copy(("c", g), cs.at[g], cr.at[g], nxt)
 
-    tiles = lax.div(c, 4) + 1
+    tiles = lax.div(c, NB) + 1
     lane = lax.broadcasted_iota(jnp.int32, (TILE, 2 * D), 1)
     gap = lax.broadcasted_iota(jnp.int32, (TILE, 2 * D), 0) - lax.rem(lane, D)
 
     def forward(g, between, after):
-        arrived(("q", g), qr.at[g])
+        arrived("q", g)
         qc = slice(g * COLS, (g + 1) * COLS)
         for h in range(WIDE):
             hc = slice(h * D, (h + 1) * D)
@@ -222,9 +230,9 @@
             qt[D:, hc] = (full - high.astype(F32)).astype(BF)
 
         def scores(j, tops):
-            xx, y0 = lax.div(j, 2), lax.rem(j, 2) * 2
+            xx = j * 2
             one = jnp.concatenate(
-                [block("k", g, n % 2, xx, y0 + n // 2) for n in range(4)], axis=0
+                [block("k", g, n % 2, xx + n // 8, n % 8 // 2) for n in range(NB)], axis=0
             )
             both = jnp.concatenate([one, one], axis=1)
             bound = c * B - j * TILE
@@ -245,9 +253,9 @@
         between()
 
         def weigh(j, _):
-            xx, y0 = lax.div(j, 2), lax.rem(j, 2) * 2
+            xx = j * 2
             one = jnp.concatenate(
-                [block("v", g, n % 2, xx, y0 + n // 2) for n in range(4)], axis=0
+                [block("v", g, n % 2, xx + n // 8, n % 8 // 2) for n in range(NB)], axis=0
             )
             left = jnp.concatenate([one.T, jnp.ones((16, TILE), BF)], axis=0)
             rows = pl.ds(pl.multiple_of(j * TILE, TILE), TILE)
@@ -261,12 +269,12 @@
         lax.fori_loop(0, tiles, weigh, 0)
         after()
         if g == 0:
-            arrived("l", lr)
+            arrived("l")
             gate_row = 1.0 / (1.0 + jnp.exp(-pick(late, lr[...], jnp.broadcast_to(lg[:, :B], (8, 128)))))
             gr[...] = gate_row
             att_acc[0] = jnp.broadcast_to(gate_row[:1], (B, D)).T
             att_acc[1] = jnp.zeros((B, D), F32)
-        arrived(("c", g), cr.at[g])
+        arrived("c", g)
         gate = att_acc[0]
         acc = att_acc[1]
         for h in range(WIDE):
@@ -282,56 +290,53 @@
 
     def backward(g):
         def terms(j, _):
-            xx, y0 = lax.div(j, 2), lax.rem(j, 2) * 2
+            xx = j * 2
             rows = pl.ds(pl.multiple_of(j * TILE, TILE), TILE)
             t = jnp.dot(wbuf[rows, :], dos[...], preferred_element_type=F32).astype(BF)
-            for n in range(4):
-                pda[g, n % 2, xx, y0 + n // 2] = t[n * B : n * B + 64]
-                pdb[g, n % 2, y0 + n // 2, xx] = t[n * B + 64 : (n + 1) * B]
+            for n in range(NB):
+                pda[g, n % 2, xx + n // 8, n % 8 // 2] = t[n * B : n * B + 64]
+                pdb[g, n % 2, n % 8 // 2, xx + n // 8] = t[n * B + 64 : (n + 1) * B]
             return 0
 
         lax.fori_loop(0, tiles, terms, 0)
 
         def blank(j, _):
-            xx, y0 = lax.div(j, 2), lax.rem(j, 2) * 2
-            for n in range(4):
-                pda[g, n % 2, xx, y0 + n // 2] = jnp.zeros((64, D), BF)
-                pdb[g, n % 2, y0 + n // 2, xx] = jnp.zeros((64, D), BF)
+            xx = j * 2
+            for n in range(NB):
+                pda[g, n % 2, xx + n // 8, n % 8 // 2] = jnp.zeros((64, D), BF)
+                pdb[g, n % 2, n % 8 // 2, xx + n // 8] = jnp.zeros((64, D), BF)
             return 0
 
-        lax.fori_loop(tiles, CTX // 4, blank, 0)
+        lax.fori_loop(tiles, CTX // NB, blank, 0)
         copy(("a0", g), pda.at[g, 1 - core], rba.at[g], sib)
-        copy(("b0", g), pdb.at[g, 1 - core], rbb.at[g], sib)
+        copy(("a0", g), pdb.at[g, 1 - core], rbb.at[g], sib)
 
     def reduce_first(g):
-        arrived(("a0", g), rba.at[g])
-        arrived(("b0", g), rbb.at[g])
+        arrived("a0", g)
         rba[g] = (pda[g, core].astype(F32) + rba[g].astype(F32)).astype(BF)
         rbb[g] = (pdb[g, core].astype(F32) + rbb[g].astype(F32)).astype(BF)
         for d in (2, 1, 3):
-            copy(("a1", g, d), rba.at[g, at(x + d)], ra.at[g, d - 1], dev(x + d, y, core))
-            copy(("b1", g, d), rbb.at[g, at(y + d)], rb.at[g, d - 1], dev(x, y + d, core))
+            copy(("a1", g), rba.at[g, at(x + d)], ra.at[g, d - 1], dev(x + d, y, core))
+            copy(("a1", g), rbb.at[g, at(y + d)], rb.at[g, d - 1], dev(x, y + d, core))
 
     def reduce_second(g):
         suma = rba[g, x].astype(F32)
         sumb = rbb[g, y].astype(F32)
+        arrived("a1", g)
         for d in (1, 3, 2):
-            arrived(("a1", g, d), ra.at[g, d - 1])
-            arrived(("b1", g, d), rb.at[g, d - 1])
             suma = suma + ra[g, d - 1].astype(F32)
             sumb = sumb + rb[g, d - 1].astype(F32)
         ua[g] = suma.astype(BF)
         ub[g] = sumb.astype(BF)
         for d in (2, 1, 3):
-            copy(("a2", g, d), ua.at[g, at(y + d)], ra2.at[g, d - 1], dev(x, y + d, core))
-            copy(("b2", g, d), ub.at[g, at(x + d)], rb2.at[g, d - 1], dev(x + d, y, core))
+            copy(("a3", g), ua.at[g, at(y + d)], ra2.at[g, d - 1], dev(x, y + d, core))
+            copy(("a3", g), ub.at[g, at(x + d)], rb2.at[g, d - 1], dev(x + d, y, core))
 
     def reduce_third(g):
         suma = ua[g, y].astype(F32)
         sumb = ub[g, x].astype(F32)
+        arrived("a3", g)
         for d in (1, 3, 2):
-            arrived(("a2", g, d), ra2.at[g, d - 1])
-            arrived(("b2", g, d), rb2.at[g, d - 1])
             suma = suma + ra2[g, d - 1].astype(F32)
             sumb = sumb + rb2[g, d - 1].astype(F32)
         kc = slice(g * D, (g + 1) * D)
@@ -341,7 +346,7 @@
 
     def hand_on(g):
         oc = slice(g * COLS, (g + 1) * COLS)
-        arrived(("h", g), hz.at[:, oc])
+        arrived("h", g)
         copy(("h2", g), hz.at[:, oc], hr.at[:, oc], prv)
 
     def gate_out():
@@ -349,32 +354,28 @@
         total = jnp.sum(att_acc[1].T, axis=0, keepdims=True)
         ls_row = gate_row * (1.0 - gate_row) * jnp.broadcast_to(total, (8, 128))
         gs[0] = ls_row
-        copy("g", gs.at[0], gs.at[1], prv)
-
-    for g in range(GROUPS):
-        gather_one(g)
-    pass_on("q", 0)
+        copy(("g",), gs.at[0], gs.at[1], prv)
+
+    gather_one(0)
     gather_second(0)
+    gather_one(1)
+    gather_third(0)
+    gather_one(2)
     gather_second(1)
     pass_on("c", 0)
-    gather_third(0)
-    gather_second(2)
     gather_fourth(0)
-    gather_second(3)
-    pass_on("q", 1)
-    gather_third(1)
+    gather_one(3)
     gather_last(0)
-    pass_on("c", 1)
     plan = {
-        (0, 0): [(pass_on2, 2), (gather_third, 2)],
-        (0, 1): [(gather_fourth, 1)],
-        (0, 2): [(gather_third, 3), (pass_on2, 3)],
-        (0, 3): [(gather_last, 1), (gather_fourth, 2)],
+        (0, 0): [(gather_third, 1), (gather_second, 2), (pass_q, 1)],
+        (0, 1): [(pass_c, 1)],
+        (0, 2): [(gather_fourth, 1), (gather_second, 3)],
+        (0, 3): [(gather_third, 2), (gather_last, 1), (pass_q, 2), (pass_c, 2)],
         (1, 0): [(reduce_first, 0)],
-        (1, 1): [(hand_on, 0), (gather_fourth, 3)],
-        (1, 2): [(gather_last, 2)],
-        (1, 3): [(reduce_second, 0)],
-        (2, 0): [(reduce_first, 1)],
+        (1, 1): [(gather_third, 3), (hand_on, 0)],
+        (1, 2): [(gather_fourth, 2), (pass_q, 3), (pass_c, 3)],
+        (1, 3): [(reduce_second, 0), (gather_last, 2)],
+        (2, 0): [(reduce_first, 1), (gather_fourth, 3)],
         (2, 1): [(reduce_third, 0), (hand_on, 1)],
         (2, 2): [(gather_last, 3)],
         (2, 3): [(reduce_second, 1)],
@@ -397,18 +398,18 @@
     last = GROUPS - 1
     reduce_first(last)
     reduce_third(2)
+    hand_on(last)
     reduce_second(last)
-    hand_on(last)
     reduce_third(last)
-    arrived("f", flr)
-    arrived("g", gs.at[1])
+    arrived("f")
+    arrived("g")
     for g in range(GROUPS):
-        arrived(("h2", g), hr.at[:, g * COLS : (g + 1) * COLS])
-        arrived(("r", g), dvr.at[:, g * D : (g + 1) * D])
+        arrived("h2", g)
+        arrived("r", g)
 
     every.wait_send()
-    for one in made:
-        one.wait_send()
+    for name in slots:
+        whole(name).wait_send()
 
 
 def finish(hz, hr, dvf, dvr, gs, fl, flr, handed, vgrad, ggrad):

time: 108 us -> 100 us (0.926)
  Pallas kernels: 106 us -> 98.9 us
    pallas_call x1, Pallas kernels: 103 us -> 95.5 us  [local(): pl.pallas_call(kernel, out_shape=(jax.ShapeDtypeStruct((B, G * COLS), BF)...]
where the time goes in v3:
time: 100 us
  Pallas kernels  98.9 us (99%)
  between operations  1.29 us (1%)
    pallas_call x1, Pallas kernels, local(): pl.pallas_call(kernel, out_shape=(jax.ShapeDtypeStruct((B, G * COLS), BF)...  95.5 us
    pallas_call x1, Pallas kernels, local(): pl.pallas_call(finish, out_shape=(jax.ShapeDtypeStruct((2 * B, G * COLS),...  3.32 us

profile of v3, /device:TPU:1, one launch (start us, length us, event | category | flops | bytes accessed | tf_op | source)
XLA Modules:
  0.0 100.2 jit_solution(16095300905298713213)
XLA Ops:
  1.3 95.5 %routed_block.1 = (bf16[128,3072]{1,0:T(8,128)(2,1)}, bf16[128,3072]{1,0:T(8,128)(2,1)}, bf16[128,512]{1,0:T(8,128)(2,1)}, bf16[128,512]{1,0:T(8,128)(2,1)}, f32...) custom-call(s32[1,1]{1,0:T(1,128)S(6)} %copy.9.counts, bf16[256,3072]{1,0:T(8,128)(2,1)} %bitcast.6, ...), custom_call_target="tpu_custom_call" | custom-call | tf_op jit(solution)/shard_map/routed_block/pallas_call | solution.py:471
  96.8 3.3 %slots.1 = (bf16[256,3072]{1,0:T(8,128)(2,1)}, bf16[256,512]{1,0:T(8,128)(2,1)}, bf16[1,256]{1,0:T(2,128)(2,1)}) custom-call(bf16[128,3072]{1,0:T(8,128)(2,1)} %get-tuple-element.13.hz, bf16[128,3072]{1,0:T(8,128)(2,1)} %get-tuple-element.14.hr, bf16[128,512]{1,0:T(8,128)(2,1)} %get-tuple-element.15.dvf, bf16[128,512]{1,0:T(8,128)(2,1)} %get-tuple-element.16.dvr, ...), custom_call_target="tpu_custom_call" | custom-call | tf_op jit(solution)/shard_map/slots/pallas_call | solution.py:490

commit v4 on v3

--- a/solution.py
+++ b/solution.py
@@ -398,8 +398,8 @@
     last = GROUPS - 1
     reduce_first(last)
     reduce_third(2)
+    reduce_second(last)
     hand_on(last)
-    reduce_second(last)
     reduce_third(last)
     arrived("f")
     arrived("g")

time: 100 us -> 100 us (level)
  no operation moved by 1% of the time
where the time goes in v4:
time: 100 us
  Pallas kernels  98.9 us (99%)
  between operations  1.29 us (1%)
    pallas_call x1, Pallas kernels, local(): pl.pallas_call(kernel, out_shape=(jax.ShapeDtypeStruct((B, G * COLS), BF)...  95.5 us
    pallas_call x1, Pallas kernels, local(): pl.pallas_call(finish, out_shape=(jax.ShapeDtypeStruct((2 * B, G * COLS),...  3.32 us

profile of v4, /device:TPU:1, one launch (start us, length us, event | category | flops | bytes accessed | tf_op | source)
XLA Modules:
  0.0 100.2 jit_solution(14577423146475132193)
XLA Ops:
  1.3 95.5 %routed_block.1 = (bf16[128,3072]{1,0:T(8,128)(2,1)}, bf16[128,3072]{1,0:T(8,128)(2,1)}, bf16[128,512]{1,0:T(8,128)(2,1)}, bf16[128,512]{1,0:T(8,128)(2,1)}, f32...) custom-call(s32[1,1]{1,0:T(1,128)S(6)} %copy.9.counts, bf16[256,3072]{1,0:T(8,128)(2,1)} %bitcast.6, ...), custom_call_target="tpu_custom_call" | custom-call | tf_op jit(solution)/shard_map/routed_block/pallas_call | solution.py:471
  96.8 3.3 %slots.1 = (bf16[256,3072]{1,0:T(8,128)(2,1)}, bf16[256,512]{1,0:T(8,128)(2,1)}, bf16[1,256]{1,0:T(2,128)(2,1)}) custom-call(bf16[128,3072]{1,0:T(8,128)(2,1)} %get-tuple-element.13.hz, bf16[128,3072]{1,0:T(8,128)(2,1)} %get-tuple-element.14.hr, bf16[128,512]{1,0:T(8,128)(2,1)} %get-tuple-element.15.dvf, bf16[128,512]{1,0:T(8,128)(2,1)} %get-tuple-element.16.dvr, ...), custom_call_target="tpu_custom_call" | custom-call | tf_op jit(solution)/shard_map/slots/pallas_call | solution.py:490
